TPU v7x, 32 devices: a 4x2x2 block of a 4x4x8 slice. The times are simulated.
32 devices in a mesh: dp: 4 (over y, z), a: 8 (over x, core).
Axes of the slice: x: 4, y: 2, z: 2, core: 2. Of those that a mesh axis runs over, the one named last changes fastest.
The devices are a block of a 4x4x8 slice.
Arguments:
- hidden_in: bfloat16 [4, 3584], P('dp'), parts along dimension 0
- loc_k: bfloat16 [4, 8, 8192, 256], P('dp', None, 'a'), parts along dimension 0
- loc_v: bfloat16 [4, 8, 8192, 256], P('dp', None, 'a'), parts along dimension 0
- glo_k: bfloat16 [4, 8, 8192, 256], P('dp', None, 'a'), parts along dimension 0
- glo_v: bfloat16 [4, 8, 8192, 256], P('dp', None, 'a'), parts along dimension 0
- loc_wq: bfloat16 [3584, 4096], P(None, 'a')
- loc_wk: bfloat16 [3584, 2048], P(None, 'a')
- loc_wv: bfloat16 [3584, 2048], P(None, 'a')
- loc_wo: bfloat16 [4096, 3584], P('a')
- loc_pre: bfloat16 [3584], replicated
- loc_post: bfloat16 [3584], replicated
- glo_wq: bfloat16 [3584, 4096], P(None, 'a')
- glo_wk: bfloat16 [3584, 2048], P(None, 'a')
- glo_wv: bfloat16 [3584, 2048], P(None, 'a')
- glo_wo: bfloat16 [4096, 3584], P('a')
- glo_pre: bfloat16 [3584], replicated
- glo_post: bfloat16 [3584], replicated
Outputs:
- output 1: bfloat16 [4, 3584], P('dp'), parts along dimension 0
- output 2: bfloat16 [4, 8, 4096, 256], P('dp', 'a'), parts along dimension 0
- output 3: bfloat16 [4, 8, 4096, 256], P('dp', 'a'), parts along dimension 0
- output 4: bfloat16 [4, 8, 8704, 256], P('dp', 'a'), parts along dimension 0
- output 5: bfloat16 [4, 8, 8704, 256], P('dp', 'a'), parts along dimension 0
There are 4 independent parts. A program takes and returns all parts, laid end to end along the dimension named above; an argument that names none is the same for every part.
All inputs are finite; a program needn't handle non-finite values.
Results may differ from a plain program's by a relative error of at most 0.02.
Values are sent between devices in bfloat16 or wider.
A program may use at most 768 MiB of HBM per device.

v0:
```python
import jax
import jax.numpy as jnp
from jax import lax
from jax.sharding import PartitionSpec as P, NamedSharding

SOFTCAP = 50.0
NORM_EPS = 1e-6
ROPE_BASE = 10000.0
WINDOW = 4096
CACHE_ROOM = 512


def rms_norm(hidden, gain):
    mean_sq = jnp.mean(hidden * hidden, axis=-1, keepdims=True)
    return hidden * lax.rsqrt(mean_sq + NORM_EPS) * (1.0 + gain.astype(jnp.float32))


def rope_at(heads, position):
    head_dim = heads.shape[-1]
    half_dim = head_dim // 2
    inv_freq = ROPE_BASE ** (-2.0 * jnp.arange(half_dim, dtype=jnp.float32) / head_dim)
    angles = position * inv_freq
    cosine = jnp.cos(angles)
    sine_val = jnp.sin(angles)
    first_half = heads[..., :half_dim]
    second_half = heads[..., half_dim:]
    return jnp.concatenate([first_half * cosine - second_half * sine_val, second_half * cosine + first_half * sine_val], axis=-1)


def attend(q_heads, old_k, old_v, new_k, new_v):
    q_scale = q_heads.shape[-1] ** -0.5
    old_scores = jnp.einsum('bkgd,bkld->bkgl', q_heads, old_k, preferred_element_type=jnp.float32) * q_scale
    new_scores = jnp.einsum('clhe,cle->clh', q_heads, new_k, preferred_element_type=jnp.float32) * q_scale
    old_scores = SOFTCAP * jnp.tanh(old_scores / SOFTCAP)
    new_scores = SOFTCAP * jnp.tanh(new_scores / SOFTCAP)
    top_score = jnp.maximum(jnp.max(old_scores, axis=-1), new_scores)
    old_weights = jnp.exp(old_scores - top_score[..., None])
    new_weights = jnp.exp(new_scores - top_score)
    denom_sum = jnp.sum(old_weights, axis=-1) + new_weights
    weighted = jnp.einsum('bkgl,bkld->bkgd', old_weights.astype(jnp.bfloat16), old_v, preferred_element_type=jnp.float32)
    weighted = weighted + new_weights.astype(jnp.bfloat16).astype(jnp.float32)[..., None] * new_v.astype(jnp.float32)[:, :, None, :]
    return weighted / denom_sum[..., None]


def decode_layer(hidden, cache_k, cache_v, w_q, w_k, w_v, w_o, pre_gain, post_gain, is_local):
    num_rows, kv_local, seq_len, head_dim = cache_k.shape
    heads_local = w_q.shape[1] // head_dim
    q_groups = heads_local // kv_local
    normed = rms_norm(hidden.astype(jnp.float32), pre_gain).astype(jnp.bfloat16)
    q_proj = jnp.dot(normed, w_q, preferred_element_type=jnp.float32)
    q_heads = rope_at(q_proj.reshape(num_rows, kv_local, q_groups, head_dim), seq_len).astype(jnp.bfloat16)
    k_proj = jnp.dot(normed, w_k, preferred_element_type=jnp.float32)
    new_k = rope_at(k_proj.reshape(num_rows, kv_local, head_dim), seq_len).astype(jnp.bfloat16)
    new_v = jnp.dot(normed, w_v, preferred_element_type=jnp.float32).astype(jnp.bfloat16).reshape(num_rows, kv_local, head_dim)
    if is_local:
        old_k = cache_k[:, :, seq_len - WINDOW + 1:]
        old_v = cache_v[:, :, seq_len - WINDOW + 1:]
        roll_shift = (seq_len + 1) % WINDOW
        out_k = jnp.roll(jnp.concatenate([old_k, new_k[:, :, None]], axis=2), roll_shift, axis=2)
        out_v = jnp.roll(jnp.concatenate([old_v, new_v[:, :, None]], axis=2), roll_shift, axis=2)
    else:
        old_k = cache_k
        old_v = cache_v
        zero_pad = jnp.zeros((num_rows, kv_local, CACHE_ROOM - 1, head_dim), jnp.bfloat16)
        out_k = jnp.concatenate([cache_k, new_k[:, :, None], zero_pad], axis=2)
        out_v = jnp.concatenate([cache_v, new_v[:, :, None], zero_pad], axis=2)
    weighted = attend(q_heads, old_k, old_v, new_k, new_v)
    attn_out = weighted.astype(jnp.bfloat16).reshape(num_rows, heads_local * head_dim)
    part_sum = jnp.dot(attn_out, w_o, preferred_element_type=jnp.float32).astype(jnp.bfloat16)
    proj_out = lax.psum(part_sum, 'a').astype(jnp.float32)
    hidden = (hidden.astype(jnp.float32) + rms_norm(proj_out, post_gain)).astype(jnp.bfloat16)
    return hidden, out_k, out_v


def solution(mesh):
    cache_in = P('dp', None, 'a', None)
    cache_out = P('dp', 'a', None, None)
    rows_spec = P('dp', None)
    layer_specs = (P(None, 'a'), P(None, 'a'), P(None, 'a'), P('a', None), P(None), P(None))
    in_specs = (rows_spec, cache_in, cache_in, cache_in, cache_in) + layer_specs + layer_specs
    out_specs = (rows_spec, cache_out, cache_out, cache_out, cache_out)

    def device_step(hidden_in, loc_k, loc_v, glo_k, glo_v, loc_wq, loc_wk, loc_wv, loc_wo, loc_pre, loc_post, glo_wq, glo_wk, glo_wv, glo_wo, glo_pre, glo_post):
        loc_k, loc_v, glo_k, glo_v = [lax.all_to_all(kv_cache, 'a', 1, 2, tiled=True) for kv_cache in (loc_k, loc_v, glo_k, glo_v)]
        hidden, loc_k_out, loc_v_out = decode_layer(hidden_in, loc_k, loc_v, loc_wq, loc_wk, loc_wv, loc_wo, loc_pre, loc_post, True)
        hidden_out, glo_k_out, glo_v_out = decode_layer(hidden, glo_k, glo_v, glo_wq, glo_wk, glo_wv, glo_wo, glo_pre, glo_post, False)
        return hidden_out, loc_k_out, loc_v_out, glo_k_out, glo_v_out

    return jax.shard_map(device_step, mesh=mesh, in_specs=in_specs, out_specs=out_specs, check_vma=False)
```

profile of v0, /device:TPU:81, one launch (start us, length us, event | category | flops | bytes accessed | tf_op | source)
XLA Modules:
  0.0 318.9 jit_solution(14625896137392270661)
XLA Ops:
  0.7 55.4 %all_to_all.48 = bf16[1,8,1024,256]{3,2,0,1:T(8,128)(2,1)} all-to-all(bf16[1,8,1024,256]{3,2,0,1:T(8,128)(2,1)} %bitcast.146), channel_id=1, replica_groups=mesh['dp'=4,'a'=8] {'a'}, dimensions={1} | all-to-all | bytes 8388608 | tf_op jit(solution)/shard_map/all_to_all | solution.py:84
  56.0 53.0 %all_to_all.49 = bf16[1,8,1024,256]{3,2,0,1:T(8,128)(2,1)} all-to-all(bf16[1,8,1024,256]{3,2,0,1:T(8,128)(2,1)S(1)} %bitcast.147), channel_id=1, replica_groups=mesh['dp'=4,'a'=8] {'a'}, dimensions={1} | all-to-all | bytes 8388608 | tf_op jit(solution)/shard_map/all_to_all | solution.py:84
  109.0 5.7 %all-to-all-start.2 = ((bf16[1,8,1024,256]{3,2,0,1:T(8,128)(2,1)}), bf16[1,8,1024,256]{3,2,0,1:T(8,128)(2,1)}, u32[]{:S(2)}, u32[]{:S(2)}) async-start(bf16[1,8,1024,256]{3,2,0,1:T(8,128)(2,1)} %bitcast.148), calls=%async_computation.2 | async-start | bytes 8388608 | tf_op jit(solution)/shard_map/all_to_all | solution.py:84
  114.8 0.6 multiply_reduce_fusion.3
  116.2 2.8 fusion.7
  118.9 0.4 convolution_bitcast_fusion.1
  119.4 0.3 fusion.44
  120.0 1.9 slice.48
  121.9 1.8 slice.51
  123.7 0.8 fusion.68
  124.6 38.8 %all-to-all-done.2 = bf16[1,8,1024,256]{3,2,0,1:T(8,128)(2,1)} async-done(((bf16[1,8,1024,256]{3,2,0,1:T(8,128)(2,1)}), bf16[1,8,1024,256]{3,2,0,1:T(8,128)(2,1)}, u32[]{:S(2)}, u32[]{:S(2)}) %all-to-all-start.2) | async-done | bytes 4194336 | tf_op jit(solution)/shard_map/all_to_all | solution.py:84
  163.4 5.6 %all-to-all-start.3 = ((bf16[1,8,1024,256]{3,2,0,1:T(8,128)(2,1)}), bf16[1,8,1024,256]{3,2,0,1:T(8,128)(2,1)}, u32[]{:S(2)}, u32[]{:S(2)}) async-start(bf16[1,8,1024,256]{3,2,0,1:T(8,128)(2,1)} %bitcast.149), calls=%async_computation.3 | async-start | bytes 8388608 | tf_op jit(solution)/shard_map/all_to_all | solution.py:84
  169.2 2.2 fusion.24
  171.4 2.8 convolution_reduce_fusion.1
  174.2 57.0 %psum.14 = bf16[1,3584]{1,0:T(2,128)(2,1)S(1)} all-reduce(bf16[1,3584]{1,0:T(2,128)(2,1)S(1)} %convert_element_type.146), channel_id=1, replica_groups=mesh['dp'=4,'a'=8] {'a'}, use_global_device_ids=true, to_apply=%region_3.4 | all-reduce | flops 3584 | bytes 14336 | tf_op jit(solution)/shard_map/psum | solution.py:70
  231.2 0.6 multiply_reduce_fusion.2
  232.5 0.6 multiply_reduce_fusion.1
  233.8 2.6 fusion.4
  236.5 0.4 convolution_bitcast_fusion
  236.9 3.6 %fusion.69 = (f32[2]{0:T(128)S(1)}, f32[2,8192]{1,0:T(2,128)S(1)}) fusion(bf16[8192,256]{1,0:T(8,128)(2,1)} %bitcast.26, bf16[2,128]{1,0:T(2,128)(2,1)S(1)} %get-tuple-element.16, bf16[2,128]{1,0:T(2,128)(2,1)S(1)} %get-tuple-element.15), kind=kOutput, calls=%fused_computation.113 | convolution fusion | flops 8439806 | bytes 4260872 | tf_op jit(solution)/shard_map/bkgd,bkld->bkgl/dot_general | solution.py:32
  240.6 0.3 fusion.34
  240.9 0.3 fusion.40
  241.3 3.0 fusion.27
  244.3 0.2 copy-done.5
  244.6 0.6 convolution_reduce_fusion
  245.2 23.7 %psum.15 = bf16[1,3584]{1,0:T(2,128)(2,1)S(1)} all-reduce(bf16[1,3584]{1,0:T(2,128)(2,1)S(1)} %convert_element_type.160), channel_id=1, replica_groups=mesh['dp'=4,'a'=8] {'a'}, use_global_device_ids=true, to_apply=%region_8.9 | all-reduce | flops 3584 | bytes 14336 | tf_op jit(solution)/shard_map/psum | solution.py:70
  268.9 0.6 multiply_reduce_fusion
  270.2 0.6 add_convert_fusion
  270.8 3.4 %pad_maximum_fusion.1 = bf16[1,1,4096,256]{3,2,1,0:T(8,128)(2,1)} fusion(bf16[1,1,4095,256]{3,2,1,0:T(8,128)(2,1)} %slice.51, bf16[1,1,1,256]{3,2,1,0:T(2,128)(2,1)S(1)} %reshape.418), kind=kLoop, calls=%fused_computation.13 | loop fusion | flops 4194304 | bytes 4194304 | tf_op jit(solution)/shard_map/jit(_roll_static)/concatenate | solution.py:60
  274.3 20.6 %concatenate.109 = bf16[1,1,8704,256]{3,2,1,0:T(8,128)(2,1)} concatenate(bf16[1,1,8192,256]{3,2,1,0:T(8,128)(2,1)} %bitcast.38, bf16[1,1,1,256]{3,2,1,0:T(2,128)(2,1)S(1)} %pad_maximum_fusion.4, bf16[1,1,511,256]{3,2,1,0:T(8,128)(2,1)S(1)} %broadcast_in_dim.14), dimensions={2} | concatenate | bytes 8912896 | tf_op jit(solution)/shard_map/concatenate | solution.py:65
  294.8 20.7 %concatenate.110 = bf16[1,1,8704,256]{3,2,1,0:T(8,128)(2,1)} concatenate(bf16[1,1,8192,256]{3,2,1,0:T(8,128)(2,1)} %bitcast.41, bf16[1,1,1,256]{3,2,1,0:T(2,128)(2,1)S(1)} %reshape.419, bf16[1,1,511,256]{3,2,1,0:T(8,128)(2,1)S(1)} %broadcast_in_dim.14), dimensions={2} | concatenate | bytes 8912896 | tf_op jit(solution)/shard_map/concatenate | solution.py:66
  315.5 3.4 %pad_maximum_fusion = bf16[1,1,4096,256]{3,2,1,0:T(8,128)(2,1)} fusion(bf16[1,1,4095,256]{3,2,1,0:T(8,128)(2,1)} %slice.48, bf16[1,1,1,128]{3,2,1,0:T(2,128)(2,1)S(1)} %bitcast.161, bf16[1,1,1,128]{3,2,1,0:T(2,128)(2,1)S(1)} %bitcast.159), kind=kLoop, calls=%fused_computation.12 | loop fusion | flops 6291456 | bytes 4194304 | tf_op jit(solution)/shard_map/jit(_roll_static)/concatenate | solution.py:59
  (58 shorter events, 1.0 us)
Async XLA Ops:
  0.6 118.3 %copy-start = (bf16[3584,256]{1,0:T(8,128)(2,1)S(1)}, bf16[3584,256]{1,0:T(8,128)(2,1)}, u32[]{:S(2)}) copy-start(bf16[3584,256]{1,0:T(8,128)(2,1)} %param.23) | copy-start | bytes 5505028
  0.6 55.4 %copy-start.4 = (bf16[1,8,1024,256]{3,2,1,0:T(8,128)(2,1)S(1)}, bf16[1,8,1024,256]{3,2,1,0:T(8,128)(2,1)}, u32[]{:S(2)}) copy-start(bf16[1,8,1024,256]{3,2,1,0:T(8,128)(2,1)} %param.19) | copy-start | bytes 12582916
  109.0 5.7 %copy-start.9 = (bf16[1,3584]{1,0:T(2,128)(2,1)S(1)}, bf16[1,3584]{1,0:T(2,128)(2,1)}, u32[]{:S(2)}) copy-start(bf16[1,3584]{1,0:T(2,128)(2,1)} %param.17) | copy-start | bytes 21508
  109.0 7.0 %copy-start.10 = (bf16[3584]{0:T(1024)(128)(2,1)S(1)}, bf16[3584]{0:T(1024)(128)(2,1)}, u32[]{:S(2)}) copy-start(bf16[3584]{0:T(1024)(128)(2,1)} %param.26) | copy-start | bytes 21508
  109.0 54.4 %all-to-all-start.2 = ((bf16[1,8,1024,256]{3,2,0,1:T(8,128)(2,1)}), bf16[1,8,1024,256]{3,2,0,1:T(8,128)(2,1)}, u32[]{:S(2)}, u32[]{:S(2)}) async-start(bf16[1,8,1024,256]{3,2,0,1:T(8,128)(2,1)} %bitcast.148), calls=%async_computation.2 | async-start | bytes 8388608 | tf_op jit(solution)/shard_map/all_to_all | solution.py:84
  116.1 3.3 %copy-start.6 = (bf16[3584,256]{1,0:T(8,128)(2,1)S(1)}, bf16[3584,256]{1,0:T(8,128)(2,1)}, u32[]{:S(2)}) copy-start(bf16[3584,256]{1,0:T(8,128)(2,1)} %param.24) | copy-start | bytes 5505028
  116.1 3.7 %copy-start.11 = (bf16[3584]{0:T(1024)(128)(2,1)S(1)}, bf16[3584]{0:T(1024)(128)(2,1)}, u32[]{:S(2)}) copy-start(bf16[3584]{0:T(1024)(128)(2,1)} %param.33) | copy-start | bytes 21508
  116.1 3.7 %copy-start.12 = (bf16[3584]{0:T(1024)(128)(2,1)S(1)}, bf16[3584]{0:T(1024)(128)(2,1)}, u32[]{:S(2)}) copy-start(bf16[3584]{0:T(1024)(128)(2,1)} %param.32) | copy-start | bytes 21508
  116.1 3.7 %copy-start.13 = (bf16[3584]{0:T(1024)(128)(2,1)S(1)}, bf16[3584]{0:T(1024)(128)(2,1)}, u32[]{:S(2)}) copy-start(bf16[3584]{0:T(1024)(128)(2,1)} %param.27) | copy-start | bytes 21508
  116.1 3.9 %copy-start.3 = (bf16[1,8,1024,256]{3,2,0,1:T(8,128)(2,1)S(1)}, bf16[1,8,1024,256]{3,2,0,1:T(8,128)(2,1)}, u32[]{:S(2)}) copy-start(bf16[1,8,1024,256]{3,2,0,1:T(8,128)(2,1)} %all_to_all.48) | copy-start | bytes 12582916
  118.9 2.9 copy-start.2
  163.4 77.9 %all-to-all-start.3 = ((bf16[1,8,1024,256]{3,2,0,1:T(8,128)(2,1)}), bf16[1,8,1024,256]{3,2,0,1:T(8,128)(2,1)}, u32[]{:S(2)}, u32[]{:S(2)}) async-start(bf16[1,8,1024,256]{3,2,0,1:T(8,128)(2,1)} %bitcast.149), calls=%async_computation.3 | async-start | bytes 8388608 | tf_op jit(solution)/shard_map/all_to_all | solution.py:84
  171.4 65.0 %copy-start.7 = (bf16[3584,256]{1,0:T(8,128)(2,1)S(1)}, bf16[3584,256]{1,0:T(8,128)(2,1)}, u32[]{:S(2)}) copy-start(bf16[3584,256]{1,0:T(8,128)(2,1)} %param.29) | copy-start | bytes 5505028
  236.4 4.5 %copy-start.8 = (bf16[3584,256]{1,0:T(8,128)(2,1)S(1)}, bf16[3584,256]{1,0:T(8,128)(2,1)}, u32[]{:S(2)}) copy-start(bf16[3584,256]{1,0:T(8,128)(2,1)} %param.30) | copy-start | bytes 5505028
  241.3 3.3 %copy-start.5 = (bf16[512,3584]{1,0:T(8,128)(2,1)S(1)}, bf16[512,3584]{1,0:T(8,128)(2,1)}, u32[]{:S(2)}) copy-start(bf16[512,3584]{1,0:T(8,128)(2,1)} %param.31) | copy-start | bytes 11010052
  294.8 24.1 %copy-start.1 = (bf16[3584,256]{1,0:T(8,128)(2,1)S(1)}, bf16[3584,256]{1,0:T(8,128)(2,1)}, u32[]{:S(2)}) copy-start(bf16[3584,256]{1,0:T(8,128)(2,1)} %param.23) | copy-start | bytes 5505028
where the time goes:
time: 322 us; the launch traced here: 319 us
  blocking collectives  189 us (59%)
  local copies, waits for them, and re-layouts  45.5 us (14%)
  waiting for transfers between devices  38.8 us (12%)
  matrix products  20 us (6%)
  starting transfers between devices  11.3 us (4%)
  other arithmetic  10.7 us (3%)
  between operations  3.7 us (1%)
    all_to_all x2, blocking collectives, device_step(): lax.all_to_all(kv_cache, 'a', 1, 2, tiled=True)  108 us
    psum x2, blocking collectives, decode_layer(): proj_out = lax.psum(part_sum, 'a').astype(jnp.float32)  80.6 us
    all_to_all x2, waiting for transfers between devices, device_step(): lax.all_to_all(kv_cache, 'a', 1, 2, tiled=True)  38.8 us
    concatenate x1, local copies, waits for them, and re-layouts, decode_layer(): out_v = jnp.concatenate([cache_v, new_v[:, :, None], zero_pad], axis=2)  20.7 us
    concatenate x1, local copies, waits for them, and re-layouts, decode_layer(): out_k = jnp.concatenate([cache_k, new_k[:, :, None], zero_pad], axis=2)  20.6 us
    all_to_all x2, starting transfers between devices, device_step(): lax.all_to_all(kv_cache, 'a', 1, 2, tiled=True)  11.3 us
  transfers between devices with their start and end apart: 2, of which 1 were waited for; matrix products, arithmetic and copies ran while one was open for 7% of the time, Pallas kernels for 0%

commit v1 on v0

v1 whole, which is shorter than its diff:
```python
import functools

import jax
import jax.numpy as jnp
import numpy as np
from jax import lax
from jax.experimental import pallas as pl
from jax.experimental.pallas import tpu as pltpu
from jax.sharding import PartitionSpec as P

SOFTCAP = 50.0
NORM_EPS = 1e-6
ROPE_BASE = 10000.0
WINDOW = 4096
CACHE_ROOM = 512
MESH = pl.DeviceIdType.MESH
CORES = 2
ROW = 512
NEG = -1e30


def rope_tables(head_dim, position):
    half = head_dim // 2
    inv = np.float32(ROPE_BASE) ** (np.float32(-2.0) * np.arange(half, dtype=np.float32) / np.float32(head_dim))
    ang = np.float32(position) * inv.astype(np.float32)
    return np.cos(ang).astype(np.float32), np.sin(ang).astype(np.float32)


def softcap(scores, scale):
    return SOFTCAP * jnp.tanh(scores * scale / SOFTCAP)


def rows_like(width):
    return lax.broadcasted_iota(jnp.int32, (8, width), 0)


class Kernel:
    def __init__(self, n, d_model, heads, blk, hd, slots):
        self.n, self.d_model, self.heads, self.blk, self.hd, self.slots = n, d_model, heads, blk, hd, slots
        self.seq = n * blk
        self.first_pos = self.seq - WINDOW + 1
        self.first_src = self.first_pos // blk
        self.chunks = d_model // ROW
        self.q_groups = 2

    def __call__(self, small, loc_k, loc_v, glo_k, glo_v, lwq, lwk, lwv, lwo, gwq, gwk, gwv, gwo,
                 hid_out, lk_out, lv_out, gk_out, gv_out,
                 wq_b, wk_b, wv_b, wo_b, kv_b, q_msg, q_all, p_msg, p_all, y_all,
                 f_sem, g_sem, d_sem, own_sem, glo_rsem, loc_rsem, w_sem, kv_sem,
                 qs_sem, qr_sem, ps_sem, pr_sem, ys_sem, yr_sem):
        n, blk, hd = self.n, self.blk, self.hd
        half = hd // 2
        me = lax.axis_index("a")
        chips = n // CORES
        chip, core = me // CORES, lax.rem(me, CORES)
        has_loc = me >= self.first_src
        right, left, opp = [lax.rem(chip + i, chips) for i in (1, chips - 1, chips // 2)]
        even = lax.rem(chip, 2) == 0
        near_f = jnp.where(even, right, left)
        near_g = jnp.where(even, left, right)

        barrier = pltpu.get_barrier_semaphore()
        for i in range(1, n):
            pl.semaphore_signal(barrier, inc=1, device_id={"a": lax.rem(me + i, n)}, device_id_type=MESH)

        weights = [((lwq, gwq), wq_b), ((lwk, gwk), wk_b), ((lwv, gwv), wv_b), ((lwo, gwo), wo_b)]
        w_cp = [[pltpu.make_async_copy(srcs[la], dst.at[la], w_sem.at[la, j]) for j, (srcs, dst) in enumerate(weights)] for la in range(2)]
        kv_cp = [[pltpu.make_async_copy(src.at[0], kv_b.at[la, j], kv_sem.at[la, j]) for j, src in enumerate(pair)]
                 for la, pair in enumerate(((loc_k, loc_v), (glo_k, glo_v)))]
        glo_pairs = ((glo_k, gk_out), (glo_v, gv_out))
        loc_pairs = ((loc_k, lk_out), (loc_v, lv_out))

        def glo_dst(out, src_dev):
            return out.at[0, 0, pl.ds(pl.multiple_of(src_dev * blk, blk), blk)]

        def loc_dst(out, src_dev):
            return out.at[0, 0, pl.ds(pl.multiple_of(lax.rem(src_dev * blk, WINDOW), blk), blk)]

        for j in range(3):
            w_cp[0][j].start()

        @pl.when(has_loc)
        def _():
            for cp in kv_cp[0]:
                cp.start()

        w_cp[0][3].start()

        pl.semaphore_wait(barrier, n - 1)

        def glo_send(kv, dst, sem):
            src, out = glo_pairs[kv]
            return pltpu.make_async_remote_copy(src_ref=src.at[0, dst], dst_ref=glo_dst(out, me), send_sem=sem,
                                                recv_sem=glo_rsem.at[kv, me], device_id={"a": dst}, device_id_type=MESH)

        def loc_send(kv, dst, sem):
            src, out = loc_pairs[kv]
            return pltpu.make_async_remote_copy(src_ref=src.at[0, dst], dst_ref=loc_dst(out, me), send_sem=sem,
                                                recv_sem=loc_rsem.at[kv, me], device_id={"a": dst}, device_id_type=MESH)

        def step_items(step):
            dst_chip = near_f if step < 4 else opp
            part = step % 4
            items = [(part % 2, dst_chip * CORES + lax.rem(core + part // 2, CORES), f_sem, step)]
            if step < 4:
                items.append((part % 2, near_g * CORES + lax.rem(core + part // 2, CORES), g_sem, step))
            return items

        def bulk_start(step):
            items = step_items(step)
            for kv, dst, sem, s in items:
                glo_send(kv, dst, sem.at[s, 0]).start()

            @pl.when(has_loc)
            def _():
                for kv, dst, sem, s in items:
                    loc_send(kv, dst, sem.at[s, 1]).start()

        def bulk_wait(step):
            items = step_items(step)
            for kv, dst, sem, s in items:
                glo_send(kv, dst, sem.at[s, 0]).wait_send()

            @pl.when(has_loc)
            def _():
                for kv, dst, sem, s in items:
                    loc_send(kv, dst, sem.at[s, 1]).wait_send()

        bulk_start(0)
        mate = chip * CORES + (CORES - 1 - core)
        own_glo = [pltpu.make_async_copy(src.at[0, me], glo_dst(out, me), own_sem.at[0, kv]) for kv, (src, out) in enumerate(glo_pairs)]
        own_loc = [pltpu.make_async_copy(src.at[0, me], loc_dst(out, me), own_sem.at[1, kv]) for kv, (src, out) in enumerate(loc_pairs)]
        for kv in range(2):
            glo_send(kv, mate, d_sem.at[0, kv]).start()
            own_glo[kv].start()

        @pl.when(has_loc)
        def _():
            for kv in range(2):
                loc_send(kv, mate, d_sem.at[1, kv]).start()
                own_loc[kv].start()

        for cp in w_cp[1] + kv_cp[1]:
            cp.start()

        def q_send(la, dst, i):
            return pltpu.make_async_remote_copy(src_ref=q_msg.at[la], dst_ref=q_all.at[la, me], send_sem=qs_sem.at[la, i - 1],
                                                recv_sem=qr_sem.at[la, me], device_id={"a": dst}, device_id_type=MESH)

        def p_send(la, dst, i):
            return pltpu.make_async_remote_copy(src_ref=p_msg.at[la, dst], dst_ref=p_all.at[la, me], send_sem=ps_sem.at[la, i - 1],
                                                recv_sem=pr_sem.at[la, me], device_id={"a": dst}, device_id_type=MESH)

        def y_send(la, dst, i):
            return pltpu.make_async_remote_copy(src_ref=y_all.at[la, me], dst_ref=y_all.at[la, me], send_sem=ys_sem.at[la, i - 1],
                                                recv_sem=yr_sem.at[la, me], device_id={"a": dst}, device_id_type=MESH)

        def q_arrival(la, src):
            return pltpu.make_async_remote_copy(src_ref=q_msg.at[la], dst_ref=q_all.at[la, src], send_sem=qs_sem.at[la, 0],
                                                recv_sem=qr_sem.at[la, src], device_id={"a": src}, device_id_type=MESH)

        def p_arrival(la, src):
            return pltpu.make_async_remote_copy(src_ref=p_msg.at[la, 0], dst_ref=p_all.at[la, src], send_sem=ps_sem.at[la, 0],
                                                recv_sem=pr_sem.at[la, src], device_id={"a": src}, device_id_type=MESH)

        def y_arrival(la, src):
            return pltpu.make_async_remote_copy(src_ref=y_all.at[la, src], dst_ref=y_all.at[la, src], send_sem=ys_sem.at[la, 0],
                                                recv_sem=yr_sem.at[la, src], device_id={"a": src}, device_id_type=MESH)

        def peers():
            return [(lax.rem(me + i, n), i) for i in range(1, n)]

        def norm(x):
            total = jnp.sum(jnp.sum(x * x, axis=1, keepdims=True), axis=0, keepdims=True)
            return x * lax.rsqrt(total / self.d_model + NORM_EPS)

        cosine = small[5, 0:1, 0:half]
        sine = small[5, 1:2, 0:half]

        def rope(x):
            first, second = x[:, :half], x[:, half:]
            return jnp.concatenate([first * cosine - second * sine, second * cosine + first * sine], axis=1)

        def round_bf16(x):
            return x.astype(jnp.bfloat16).astype(jnp.float32)

        def project(la, hidden, gain):
            a = norm(hidden) * (1.0 + gain)
            for j in range(3):
                w_cp[la][j].wait()
            q = k = v = None
            for i in range(self.chunks):
                lhs = jnp.broadcast_to(a[i:i + 1, :], (16, ROW)).astype(jnp.bfloat16)
                part = [jnp.dot(lhs, w[la, i * ROW:(i + 1) * ROW, :], preferred_element_type=jnp.float32) for w in (wq_b, wk_b, wv_b)]
                q, k, v = part if q is None else (q + part[0], k + part[1], v + part[2])
            q, k, v = q[:8], k[:8], v[:8]
            q0, q1 = rope(q[:, :hd]), rope(q[:, hd:])
            q = round_bf16(jnp.where(rows_like(hd) == 0, q0, q1))
            return q, round_bf16(rope(k)), round_bf16(v)

        def attend_block(la, h, masked):
            q = q_all[la, h].astype(jnp.bfloat16)
            s = lax.dot_general(q, kv_b[la, 0, h], (((1,), (1,)), ((), ())), preferred_element_type=jnp.float32)
            s = softcap(s, hd ** -0.5)
            if masked:
                pos = me * blk + lax.broadcasted_iota(jnp.int32, s.shape, 1)
                s = jnp.where(pos >= self.first_pos, s, NEG)
            top = jnp.max(s, axis=1, keepdims=True)
            e = jnp.exp(s - top)
            if masked:
                e = jnp.where(pos >= self.first_pos, e, 0.0)
            total = jnp.sum(e, axis=1, keepdims=True)
            o = jnp.dot(e.astype(jnp.bfloat16), kv_b[la, 1, h], preferred_element_type=jnp.float32)
            lane = lax.broadcasted_iota(jnp.int32, (8, 128), 1)
            p_msg[la, h, :, 0:hd] = o
            p_msg[la, h, :, hd:hd + 128] = jnp.where(lane < 64, top, total)

        def attend_all(la, masked):
            for cp in kv_cp[la]:
                cp.wait()

            def body(h, carry):
                attend_block(la, h, masked)
                return carry

            lax.fori_loop(0, n, body, 0)
            for dst, i in peers():
                p_send(la, dst, i).start()
            p_all[la, me] = p_msg[la, me]

        def combine(la, q, k_new, v_new, first_src):
            s_new = softcap(jnp.sum(q * k_new, axis=1, keepdims=True), hd ** -0.5)
            tops = [p_all[la, s, :, hd:hd + 1] for s in range(first_src, n)]
            sums = [p_all[la, s, :, hd + 64:hd + 65] for s in range(first_src, n)]
            top = s_new
            for t in tops:
                top = jnp.maximum(top, t)
            e_new = jnp.exp(s_new - top)
            denom = e_new
            o = round_bf16(e_new) * v_new
            for idx, s in enumerate(range(first_src, n)):
                w = jnp.exp(tops[idx] - top)
                denom = denom + w * sums[idx]
                o = o + w * p_all[la, s, :, 0:hd]
            return o / denom

        def out_project(la, o):
            w_cp[la][3].wait()
            lhs = [jnp.broadcast_to(o[g:g + 1, :], (16, hd)).astype(jnp.bfloat16) for g in range(self.q_groups)]
            row = rows_like(ROW)
            msg = jnp.zeros((8, ROW), jnp.float32)
            for i in range(self.chunks):
                y = None
                for g in range(self.q_groups):
                    part = jnp.dot(lhs[g], wo_b[la, g * hd:(g + 1) * hd, i * ROW:(i + 1) * ROW], preferred_element_type=jnp.float32)
                    y = part if y is None else y + part
                msg = jnp.where(row == i, y[:8], msg)
            y_all[la, me] = msg
            for dst, i in peers():
                y_send(la, dst, i).start()

        hidden = small[0]
        fresh = []
        for la in range(2):
            pre, post = small[1 + 2 * la], small[2 + 2 * la]
            q, k_new, v_new = project(la, hidden, pre)
            fresh.append((k_new, v_new))
            q_msg[la] = q
            q_all[la, me] = q
            for dst, i in peers():
                q_send(la, dst, i).start()
            step = 3 * la + 1
            bulk_start(step)
            bulk_wait(step - 1)
            for src, i in peers():
                q_arrival(la, src).wait_recv()
            if la == 0:
                @pl.when(has_loc)
                def _():
                    attend_all(0, True)
            else:
                attend_all(1, False)
            bulk_start(step + 1)
            bulk_wait(step)
            first_src = self.first_src if la == 0 else 0
            for src, i in peers():
                if la == 0:
                    @pl.when(src >= first_src)
                    def _():
                        p_arrival(0, src).wait_recv()
                else:
                    p_arrival(la, src).wait_recv()
            out_project(la, combine(la, q, k_new, v_new, first_src))
            bulk_start(step + 2)
            bulk_wait(step + 1)
            for src, i in peers():
                y_arrival(la, src).wait_recv()
            y = y_all[la, 0]
            for s in range(1, n):
                y = y + y_all[la, s]
            hidden = round_bf16(hidden + norm(y) * (1.0 + post))
        for i in range(self.chunks):
            hid_out[:, i * ROW:(i + 1) * ROW] = hidden[i:i + 1, :].astype(jnp.bfloat16)

        bulk_start(7)
        row16 = lax.broadcasted_iota(jnp.int32, (16, hd), 0)
        for kv, out in enumerate((gk_out, gv_out)):
            new = jnp.concatenate([fresh[1][kv], fresh[1][kv]], axis=0)
            out[0, 0, self.seq:self.seq + 16, :] = jnp.where(row16 == 0, new, 0.0).astype(jnp.bfloat16)
            out[0, 0, self.seq + 16:self.slots, :] = jnp.zeros((self.slots - self.seq - 16, hd), jnp.bfloat16)

        for la in range(2):
            for dst, i in peers():
                q_send(la, dst, i).wait_send()
                y_send(la, dst, i).wait_send()
        for dst, i in peers():
            p_send(1, dst, i).wait_send()

        @pl.when(has_loc)
        def _():
            for dst, i in peers():
                p_send(0, dst, i).wait_send()
            for kv in range(2):
                loc_send(kv, mate, d_sem.at[1, kv]).wait_send()
                own_loc[kv].wait()

        for kv in range(2):
            glo_send(kv, mate, d_sem.at[0, kv]).wait_send()
            own_glo[kv].wait()

        def glo_arrival(kv, src_dev):
            src, out = glo_pairs[kv]
            return pltpu.make_async_remote_copy(src_ref=src.at[0, 0], dst_ref=glo_dst(out, src_dev), send_sem=d_sem.at[0, kv],
                                                recv_sem=glo_rsem.at[kv, src_dev], device_id={"a": src_dev}, device_id_type=MESH)

        def loc_arrival(kv, src_dev):
            src, out = loc_pairs[kv]
            return pltpu.make_async_remote_copy(src_ref=src.at[0, 0], dst_ref=loc_dst(out, src_dev), send_sem=d_sem.at[1, kv],
                                                recv_sem=loc_rsem.at[kv, src_dev], device_id={"a": src_dev}, device_id_type=MESH)

        for src_dev, i in peers():
            @pl.when(src_dev >= self.first_src)
            def _():
                for kv in range(2):
                    loc_arrival(kv, src_dev).wait_recv()
        slot = (self.seq % WINDOW) // 16 * 16
        for kv, out in enumerate((lk_out, lv_out)):
            new = jnp.concatenate([fresh[0][kv], fresh[0][kv]], axis=0)
            old = out[0, 0, slot:slot + 16, :].astype(jnp.float32)
            out[0, 0, slot:slot + 16, :] = jnp.where(row16 == self.seq % WINDOW - slot, new, old).astype(jnp.bfloat16)

        bulk_wait(6)
        bulk_wait(7)
        for src_dev, i in peers():
            for kv in range(2):
                glo_arrival(kv, src_dev).wait_recv()


def solution(mesh):
    n = mesh.shape["a"]
    cache_in = P("dp", None, "a", None)
    cache_out = P("dp", "a", None, None)
    rows_spec = P("dp", None)
    layer_specs = (P(None, "a"), P(None, "a"), P(None, "a"), P("a", None), P(None), P(None))
    in_specs = (rows_spec, cache_in, cache_in, cache_in, cache_in) + layer_specs + layer_specs
    out_specs = (rows_spec, cache_out, cache_out, cache_out, cache_out)

    def device_step(hidden_in, loc_k, loc_v, glo_k, glo_v, loc_wq, loc_wk, loc_wv, loc_wo, loc_pre, loc_post, glo_wq, glo_wk, glo_wv, glo_wo, glo_pre, glo_post):
        d_model = hidden_in.shape[1]
        rows, heads, blk, hd = loc_k.shape
        q_cols, kv_cols = loc_wq.shape[1], loc_wk.shape[1]
        seq = n * blk
        slots = seq + CACHE_ROOM
        pad = 8 * ROW - d_model

        def tile(x):
            return jnp.pad(x.astype(jnp.float32).reshape(-1), (0, 8 * ROW - x.size)).reshape(8, ROW)

        cosine, sine = rope_tables(hd, seq)
        table = np.zeros((8, ROW), np.float32)
        table[0, :hd // 2], table[1, :hd // 2] = cosine, sine
        small = jnp.stack([tile(hidden_in), tile(loc_pre), tile(loc_post), tile(glo_pre), tile(glo_post), jnp.asarray(table)])

        vmem = pl.BlockSpec(memory_space=pltpu.VMEM)
        hbm = pl.BlockSpec(memory_space=pltpu.HBM)
        bf16, f32 = jnp.bfloat16, jnp.float32
        dma = pltpu.SemaphoreType.DMA
        return pl.pallas_call(
            Kernel(n, d_model, heads, blk, hd, slots),
            name="decode_step",
            out_shape=(
                jax.ShapeDtypeStruct(hidden_in.shape, bf16),
                pltpu.VMEM((rows, 1, WINDOW, hd), bf16),
                pltpu.VMEM((rows, 1, WINDOW, hd), bf16),
                pltpu.VMEM((rows, 1, slots, hd), bf16),
                pltpu.VMEM((rows, 1, slots, hd), bf16),
            ),
            in_specs=[vmem] + [hbm] * 12,
            out_specs=(vmem,) * 5,
            scratch_shapes=[
                pltpu.VMEM((2, d_model, q_cols), bf16),
                pltpu.VMEM((2, d_model, kv_cols), bf16),
                pltpu.VMEM((2, d_model, kv_cols), bf16),
                pltpu.VMEM((2, q_cols, d_model), bf16),
                pltpu.VMEM((2, 2, heads, blk, hd), bf16),
                pltpu.VMEM((2, 8, hd), f32),
                pltpu.VMEM((2, n, 8, hd), f32),
                pltpu.VMEM((2, n, 8, hd + 128), f32),
                pltpu.VMEM((2, n, 8, hd + 128), f32),
                pltpu.VMEM((2, n, 8, ROW), f32),
                dma((8, 2)), dma((4, 2)), dma((2, 2)), dma((2, 2)), dma((2, n)), dma((2, n)), dma((2, 4)), dma((2, 2)),
                dma((2, n - 1)), dma((2, n)), dma((2, n - 1)), dma((2, n)), dma((2, n - 1)), dma((2, n)),
            ],
            compiler_params=pltpu.CompilerParams(collective_id=0, has_side_effects=True, vmem_limit_bytes=48 * 2**20),
        )(small, loc_k, loc_v, glo_k, glo_v, loc_wq, loc_wk, loc_wv, loc_wo, glo_wq, glo_wk, glo_wv, glo_wo)

    return jax.shard_map(device_step, mesh=mesh, in_specs=in_specs, out_specs=out_specs, check_vma=False)
```

time: 322 us -> 209 us (0.65)
  Pallas kernels: 0 us -> 196 us
  blocking collectives: 189 us -> 0 us
  waiting for transfers between devices: 38.8 us -> 0 us
  local copies, waits for them, and re-layouts: 45.5 us -> 8.85 us
  matrix products: 20 us -> 0 us
  starting transfers between devices: 11.3 us -> 0 us
  other arithmetic: 10.7 us -> 3.57 us
    pallas_call x0 -> x1, Pallas kernels: none -> 196 us  [device_step(): pl.pallas_call(Kernel(n, d_model, heads, blk, hd, slots), name='decode_st...]
    all_to_all x2 -> x0, blocking collectives: 108 us -> none  [device_step(): lax.all_to_all(kv_cache, 'a', 1, 2, tiled=True)]
    psum x2 -> x0, blocking collectives: 80.6 us -> none  [decode_layer(): proj_out = lax.psum(part_sum, 'a').astype(jnp.float32)]
    concatenate x4 -> x0, local copies, waits for them, and re-layouts: 41.3 us -> none  [the longest x1 20.7 us: decode_layer(): out_v = jnp.concatenate([cache_v, new_v[:, :, None], zero_pad], axis=2)]
    all_to_all x2 -> x0, waiting for transfers between devices: 38.8 us -> none  [device_step(): lax.all_to_all(kv_cache, 'a', 1, 2, tiled=True)]
    dot_general x14 -> x0, matrix products: 20 us -> none  [the longest x2 5.37 us: decode_layer(): q_proj = jnp.dot(normed, w_q, preferred_element_type=jnp.float32)]
    all_to_all x2 -> x0, starting transfers between devices: 11.3 us -> none  [device_step(): lax.all_to_all(kv_cache, 'a', 1, 2, tiled=True)]
    unnamed x30 -> x14, local copies, waits for them, and re-layouts: 0.44 us -> 8.1 us
  transfers between devices with their start and end apart: 2 -> 0, of which waited for: 1 -> 0; matrix products, arithmetic and copies ran while one was open for 7% -> 0% of each run, Pallas kernels for 0% -> 0%
where the time goes in v1:
time: 209 us
  Pallas kernels  196 us (94%)
  local copies, waits for them, and re-layouts  8.85 us (4%)
  other arithmetic  3.57 us (2%)
    pallas_call x1, Pallas kernels, device_step(): pl.pallas_call(Kernel(n, d_model, heads, blk, hd, slots), name='decode_st...  196 us
    unnamed x14, local copies, waits for them, and re-layouts  8.1 us

profile of v1, /device:TPU:81, one launch (start us, length us, event | category | flops | bytes accessed | tf_op | source)
XLA Modules:
  0.0 208.9 jit_solution(14071844861935949922)
XLA Ops:
  0.6 0.8 reduce
  1.4 0.7 pad_convert_fusion.3
  2.1 0.7 pad_convert_fusion.2
  2.8 0.7 pad_convert_fusion.1
  3.5 0.7 pad_convert_fusion
  4.3 0.7 constant_dynamic-update-slice_fusion.small
  5.0 0.0 copy-start
  5.0 0.6 copy-done
  5.7 195.8 %decode_step.1 = (bf16[1,3584]{1,0:T(2,128)(2,1)}, bf16[1,1,4096,256]{3,2,1,0:T(8,128)(2,1)S(1)}, bf16[1,1,4096,256]{3,2,1,0:T(8,128)(2,1)S(1)}, bf16[1,1,8704,2...) custom-call(f32[6,8,512]{2,1,0:T(8,128)} %copy-done, bf16[1,8,1024,256]{3,2,1,0:T(8,128)(2,1)} %loc_k.1, ...), custom_call_target="tpu_custom_call" | custom-call | tf_op jit(solution)/shard_map/decode_step/pallas_call | solution.py:388
  201.5 1.3 copy.33
  202.8 1.3 copy.34
  204.1 2.1 %copy.35 = bf16[1,1,8704,256]{3,2,1,0:T(8,128)(2,1)} copy(bf16[1,1,8704,256]{3,2,1,0:T(8,128)(2,1)S(1)} %get-tuple-element.8) | data formatting | bytes 8912896
  206.2 0.0 copy-start.1
  206.2 2.1 %copy.36 = bf16[1,1,8704,256]{3,2,1,0:T(8,128)(2,1)} copy(bf16[1,1,8704,256]{3,2,1,0:T(8,128)(2,1)S(1)} %get-tuple-element.9) | data formatting | bytes 8912896
  208.3 0.0 copy-done.1
  208.3 0.6 copy.37
  (11 shorter events, 0.1 us)
Async XLA Ops:
  5.0 0.6 copy-start
  206.2 2.1 %copy-start.1 = (bf16[1,3584]{1,0:T(2,128)(2,1)S(1)}, bf16[1,3584]{1,0:T(2,128)(2,1)}, u32[]{:S(2)}) copy-start(bf16[1,3584]{1,0:T(2,128)(2,1)} %get-tuple-element.15) | copy-start | bytes 21508

commit v2 on v1

--- a/solution.py
+++ b/solution.py
@@ -16,6 +16,7 @@
 MESH = pl.DeviceIdType.MESH
 CORES = 2
 ROW = 512
+STORE_PARTS = 4
 NEG = -1e30
 
 
@@ -32,6 +33,20 @@
 
 def rows_like(width):
     return lax.broadcasted_iota(jnp.int32, (8, width), 0)
+
+
+def store_outputs(*refs):
+    landed, outs, sem = refs[:5], refs[5:10], refs[10]
+    copies = [pltpu.make_async_copy(landed[0], outs[0], sem.at[0, 0])]
+    for j in range(1, 5):
+        part = landed[j].shape[2] // STORE_PARTS
+        for p in range(STORE_PARTS):
+            rows = pl.ds(p * part, part)
+            copies.append(pltpu.make_async_copy(landed[j].at[0, 0, rows], outs[j].at[0, 0, rows], sem.at[j, p]))
+    for cp in copies:
+        cp.start()
+    for cp in copies:
+        cp.wait()
 
 
 class Kernel:
@@ -43,10 +58,10 @@
         self.chunks = d_model // ROW
         self.q_groups = 2
 
-    def __call__(self, small, loc_k, loc_v, glo_k, glo_v, lwq, lwk, lwv, lwo, gwq, gwk, gwv, gwo,
+    def __call__(self, hid_in, table_in, loc_k, loc_v, glo_k, glo_v, lwq, lwk, lwv, lwo, lpre, lpost, gwq, gwk, gwv, gwo, gpre, gpost,
                  hid_out, lk_out, lv_out, gk_out, gv_out,
-                 wq_b, wk_b, wv_b, wo_b, kv_b, q_msg, q_all, p_msg, p_all, y_all,
-                 f_sem, g_sem, d_sem, own_sem, glo_rsem, loc_rsem, w_sem, kv_sem,
+                 hid_b, table, gain_b, wq_b, wk_b, wv_b, wo_b, kv_b, q_msg, q_all, p_msg, p_all, y_all,
+                 in_sem, f_sem, g_sem, d_sem, own_sem, glo_rsem, loc_rsem, w_sem, kv_sem,
                  qs_sem, qr_sem, ps_sem, pr_sem, ys_sem, yr_sem):
         n, blk, hd = self.n, self.blk, self.hd
         half = hd // 2
@@ -76,8 +91,10 @@
         def loc_dst(out, src_dev):
             return out.at[0, 0, pl.ds(pl.multiple_of(lax.rem(src_dev * blk, WINDOW), blk), blk)]
 
-        for j in range(3):
-            w_cp[0][j].start()
+        in_cp = [pltpu.make_async_copy(hid_in, hid_b, in_sem.at[0]), pltpu.make_async_copy(table_in, table, in_sem.at[1])]
+        in_cp += [pltpu.make_async_copy(g, b, in_sem.at[2 + j]) for j, (g, b) in enumerate(zip((lpre, lpost, gpre, gpost), gain_b))]
+        for cp in in_cp + w_cp[0][:3]:
+            cp.start()
 
         @pl.when(has_loc)
         def _():
@@ -140,8 +157,8 @@
                 loc_send(kv, mate, d_sem.at[1, kv]).start()
                 own_loc[kv].start()
 
-        for cp in w_cp[1] + kv_cp[1]:
-            cp.start()
+        for cp in in_cp:
+            cp.wait()
 
         def q_send(la, dst, i):
             return pltpu.make_async_remote_copy(src_ref=q_msg.at[la], dst_ref=q_all.at[la, me], send_sem=qs_sem.at[la, i - 1],
@@ -174,8 +191,17 @@
             total = jnp.sum(jnp.sum(x * x, axis=1, keepdims=True), axis=0, keepdims=True)
             return x * lax.rsqrt(total / self.d_model + NORM_EPS)
 
-        cosine = small[5, 0:1, 0:half]
-        sine = small[5, 1:2, 0:half]
+        cosine, sine = table[0:1, :], table[1:2, :]
+
+        def tiled(piece):
+            row = rows_like(ROW)
+            out = jnp.zeros((8, ROW), jnp.float32)
+            for i in range(self.chunks):
+                out = jnp.where(row == i, piece(i), out)
+            return out
+
+        def gain(j):
+            return tiled(lambda i: gain_b[j][i * ROW:(i + 1) * ROW].astype(jnp.float32).reshape(1, ROW))
 
         def rope(x):
             first, second = x[:, :half], x[:, half:]
@@ -184,8 +210,8 @@
         def round_bf16(x):
             return x.astype(jnp.bfloat16).astype(jnp.float32)
 
-        def project(la, hidden, gain):
-            a = norm(hidden) * (1.0 + gain)
+        def project(la, hidden, pre):
+            a = norm(hidden) * (1.0 + pre)
             for j in range(3):
                 w_cp[la][j].wait()
             q = k = v = None
@@ -193,9 +219,9 @@
                 lhs = jnp.broadcast_to(a[i:i + 1, :], (16, ROW)).astype(jnp.bfloat16)
                 part = [jnp.dot(lhs, w[la, i * ROW:(i + 1) * ROW, :], preferred_element_type=jnp.float32) for w in (wq_b, wk_b, wv_b)]
                 q, k, v = part if q is None else (q + part[0], k + part[1], v + part[2])
-            q, k, v = q[:8], k[:8], v[:8]
+            q, k, v = q[:2], k[:2], v[:2]
             q0, q1 = rope(q[:, :hd]), rope(q[:, hd:])
-            q = round_bf16(jnp.where(rows_like(hd) == 0, q0, q1))
+            q = round_bf16(jnp.where(lax.broadcasted_iota(jnp.int32, (2, hd), 0) == 0, q0, q1))
             return q, round_bf16(rope(k)), round_bf16(v)
 
         def attend_block(la, h, masked):
@@ -211,7 +237,7 @@
                 e = jnp.where(pos >= self.first_pos, e, 0.0)
             total = jnp.sum(e, axis=1, keepdims=True)
             o = jnp.dot(e.astype(jnp.bfloat16), kv_b[la, 1, h], preferred_element_type=jnp.float32)
-            lane = lax.broadcasted_iota(jnp.int32, (8, 128), 1)
+            lane = lax.broadcasted_iota(jnp.int32, (2, 128), 1)
             p_msg[la, h, :, 0:hd] = o
             p_msg[la, h, :, hd:hd + 128] = jnp.where(lane < 64, top, total)
 
@@ -255,14 +281,14 @@
                     part = jnp.dot(lhs[g], wo_b[la, g * hd:(g + 1) * hd, i * ROW:(i + 1) * ROW], preferred_element_type=jnp.float32)
                     y = part if y is None else y + part
                 msg = jnp.where(row == i, y[:8], msg)
-            y_all[la, me] = msg
+            y_all[la, me] = msg.astype(jnp.bfloat16)
             for dst, i in peers():
                 y_send(la, dst, i).start()
 
-        hidden = small[0]
+        hidden = tiled(lambda i: hid_b[:, i * ROW:(i + 1) * ROW].astype(jnp.float32))
         fresh = []
         for la in range(2):
-            pre, post = small[1 + 2 * la], small[2 + 2 * la]
+            pre, post = gain(2 * la), gain(2 * la + 1)
             q, k_new, v_new = project(la, hidden, pre)
             fresh.append((k_new, v_new))
             q_msg[la] = q
@@ -272,6 +298,9 @@
             step = 3 * la + 1
             bulk_start(step)
             bulk_wait(step - 1)
+            if la == 0:
+                for cp in w_cp[1] + kv_cp[1]:
+                    cp.start()
             for src, i in peers():
                 q_arrival(la, src).wait_recv()
             if la == 0:
@@ -295,9 +324,9 @@
             bulk_wait(step + 1)
             for src, i in peers():
                 y_arrival(la, src).wait_recv()
-            y = y_all[la, 0]
+            y = y_all[la, 0].astype(jnp.float32)
             for s in range(1, n):
-                y = y + y_all[la, s]
+                y = y + y_all[la, s].astype(jnp.float32)
             hidden = round_bf16(hidden + norm(y) * (1.0 + post))
         for i in range(self.chunks):
             hid_out[:, i * ROW:(i + 1) * ROW] = hidden[i:i + 1, :].astype(jnp.bfloat16)
@@ -305,7 +334,7 @@
         bulk_start(7)
         row16 = lax.broadcasted_iota(jnp.int32, (16, hd), 0)
         for kv, out in enumerate((gk_out, gv_out)):
-            new = jnp.concatenate([fresh[1][kv], fresh[1][kv]], axis=0)
+            new = jnp.broadcast_to(fresh[1][kv][0:1], (16, hd))
             out[0, 0, self.seq:self.seq + 16, :] = jnp.where(row16 == 0, new, 0.0).astype(jnp.bfloat16)
             out[0, 0, self.seq + 16:self.slots, :] = jnp.zeros((self.slots - self.seq - 16, hd), jnp.bfloat16)
 
@@ -345,7 +374,7 @@
                     loc_arrival(kv, src_dev).wait_recv()
         slot = (self.seq % WINDOW) // 16 * 16
         for kv, out in enumerate((lk_out, lv_out)):
-            new = jnp.concatenate([fresh[0][kv], fresh[0][kv]], axis=0)
+            new = jnp.broadcast_to(fresh[0][kv][0:1], (16, hd))
             old = out[0, 0, slot:slot + 16, :].astype(jnp.float32)
             out[0, 0, slot:slot + 16, :] = jnp.where(row16 == self.seq % WINDOW - slot, new, old).astype(jnp.bfloat16)
 
@@ -371,47 +400,51 @@
         q_cols, kv_cols = loc_wq.shape[1], loc_wk.shape[1]
         seq = n * blk
         slots = seq + CACHE_ROOM
-        pad = 8 * ROW - d_model
-
-        def tile(x):
-            return jnp.pad(x.astype(jnp.float32).reshape(-1), (0, 8 * ROW - x.size)).reshape(8, ROW)
-
-        cosine, sine = rope_tables(hd, seq)
-        table = np.zeros((8, ROW), np.float32)
-        table[0, :hd // 2], table[1, :hd // 2] = cosine, sine
-        small = jnp.stack([tile(hidden_in), tile(loc_pre), tile(loc_post), tile(glo_pre), tile(glo_post), jnp.asarray(table)])
+        table = jnp.asarray(np.stack(rope_tables(hd, seq)))
 
         vmem = pl.BlockSpec(memory_space=pltpu.VMEM)
         hbm = pl.BlockSpec(memory_space=pltpu.HBM)
         bf16, f32 = jnp.bfloat16, jnp.float32
         dma = pltpu.SemaphoreType.DMA
-        return pl.pallas_call(
+        landed = pl.pallas_call(
             Kernel(n, d_model, heads, blk, hd, slots),
             name="decode_step",
             out_shape=(
-                jax.ShapeDtypeStruct(hidden_in.shape, bf16),
+                pltpu.VMEM(hidden_in.shape, bf16),
                 pltpu.VMEM((rows, 1, WINDOW, hd), bf16),
                 pltpu.VMEM((rows, 1, WINDOW, hd), bf16),
                 pltpu.VMEM((rows, 1, slots, hd), bf16),
                 pltpu.VMEM((rows, 1, slots, hd), bf16),
             ),
-            in_specs=[vmem] + [hbm] * 12,
+            in_specs=[hbm] * 18,
             out_specs=(vmem,) * 5,
             scratch_shapes=[
+                pltpu.VMEM(hidden_in.shape, bf16),
+                pltpu.VMEM((2, hd // 2), f32),
+                [pltpu.VMEM((d_model,), bf16)] * 4,
                 pltpu.VMEM((2, d_model, q_cols), bf16),
                 pltpu.VMEM((2, d_model, kv_cols), bf16),
                 pltpu.VMEM((2, d_model, kv_cols), bf16),
                 pltpu.VMEM((2, q_cols, d_model), bf16),
                 pltpu.VMEM((2, 2, heads, blk, hd), bf16),
-                pltpu.VMEM((2, 8, hd), f32),
-                pltpu.VMEM((2, n, 8, hd), f32),
-                pltpu.VMEM((2, n, 8, hd + 128), f32),
-                pltpu.VMEM((2, n, 8, hd + 128), f32),
-                pltpu.VMEM((2, n, 8, ROW), f32),
-                dma((8, 2)), dma((4, 2)), dma((2, 2)), dma((2, 2)), dma((2, n)), dma((2, n)), dma((2, 4)), dma((2, 2)),
+                pltpu.VMEM((2, 2, hd), f32),
+                pltpu.VMEM((2, n, 2, hd), f32),
+                pltpu.VMEM((2, n, 2, hd + 128), f32),
+                pltpu.VMEM((2, n, 2, hd + 128), f32),
+                pltpu.VMEM((2, n, 8, ROW), bf16),
+                dma((6,)), dma((8, 2)), dma((4, 2)), dma((2, 2)), dma((2, 2)), dma((2, n)), dma((2, n)), dma((2, 4)), dma((2, 2)),
                 dma((2, n - 1)), dma((2, n)), dma((2, n - 1)), dma((2, n)), dma((2, n - 1)), dma((2, n)),
             ],
             compiler_params=pltpu.CompilerParams(collective_id=0, has_side_effects=True, vmem_limit_bytes=48 * 2**20),
-        )(small, loc_k, loc_v, glo_k, glo_v, loc_wq, loc_wk, loc_wv, loc_wo, glo_wq, glo_wk, glo_wv, glo_wo)
+        )(hidden_in, table, loc_k, loc_v, glo_k, glo_v, loc_wq, loc_wk, loc_wv, loc_wo, loc_pre, loc_post, glo_wq, glo_wk, glo_wv, glo_wo, glo_pre, glo_post)
+        return pl.pallas_call(
+            store_outputs,
+            name="store_outputs",
+            out_shape=tuple(jax.ShapeDtypeStruct(x.shape, x.dtype) for x in landed),
+            in_specs=[vmem] * 5,
+            out_specs=(hbm,) * 5,
+            scratch_shapes=[dma((5, STORE_PARTS))],
+            compiler_params=pltpu.CompilerParams(vmem_limit_bytes=2**20),
+        )(*landed)
 
     return jax.shard_map(device_step, mesh=mesh, in_specs=in_specs, out_specs=out_specs, check_vma=False)

time: 209 us -> 196 us (0.938)
  local copies, waits for them, and re-layouts: 8.85 us -> 0 us
  other arithmetic: 3.57 us -> 0 us
    unnamed x14 -> x0, local copies, waits for them, and re-layouts: 8.1 us -> none
    pallas_call x1, Pallas kernels: 196 us -> 191 us  [device_step(): pl.pallas_call(Kernel(n, d_model, heads, blk, hd, slots), name='decode_st...]
    pallas_call x0 -> x1, Pallas kernels: none -> 4.9 us  [device_step(): pl.pallas_call(store_outputs, name='store_outputs', out_shape=tuple((jax....]
    another operation x5 -> x0, other arithmetic: 2.81 us -> none  [device_step(): jnp.stack([tile(hidden_in), tile(loc_pre), tile(loc_post), tile(glo_pre),...]
where the time goes in v2:
time: 196 us
  Pallas kernels  195 us (99%)
    pallas_call x1, Pallas kernels, device_step(): pl.pallas_call(Kernel(n, d_model, heads, blk, hd, slots), name='decode_st...  191 us
    pallas_call x1, Pallas kernels, device_step(): pl.pallas_call(store_outputs, name='store_outputs', out_shape=tuple((jax....  4.9 us

profile of v2, /device:TPU:81, one launch (start us, length us, event | category | flops | bytes accessed | tf_op | source)
XLA Modules:
  0.0 196.1 jit_solution(16893309553815884797)
XLA Ops:
  0.6 190.5 %decode_step.1 = (bf16[1,3584]{1,0:T(2,128)(2,1)S(1)}, bf16[1,1,4096,256]{3,2,1,0:T(8,128)(2,1)S(1)}, bf16[1,1,4096,256]{3,2,1,0:T(8,128)(2,1)S(1)}, bf16[1,1,87...) custom-call(bf16[1,3584]{1,0:T(2,128)(2,1)} %hid_in.1, f32[2,128]{1,0:T(2,128)} %constant.2.clone.table_in, ...), custom_call_target="tpu_custom_call" | custom-call | tf_op jit(solution)/shard_map/decode_step/pallas_call | solution.py:409
  191.2 4.9 %store_outputs.1 = (bf16[1,3584]{1,0:T(2,128)(2,1)}, bf16[1,1,4096,256]{3,2,1,0:T(8,128)(2,1)}, bf16[1,1,4096,256]{3,2,1,0:T(8,128)(2,1)}, bf16[1,1,8704,256]{3,2,1,0:T(8,128)(2,1)}, bf16[1,1,8704,256]{3,2,1,0:T(8,128)(2,1)}) custom-call(bf16[1,3584]{1,0:T(2,128)(2,1)S(1)} %get-tuple-element.10.refs_0_, ...), custom_call_target="tpu_custom_call" | custom-call | tf_op jit(solution)/shard_map/store_outputs/pallas_call | solution.py:440

commit v3 on v2

--- a/solution.py
+++ b/solution.py
@@ -16,7 +16,8 @@
 MESH = pl.DeviceIdType.MESH
 CORES = 2
 ROW = 512
-STORE_PARTS = 4
+STORE_PARTS = 2
+RELAY = 96
 NEG = -1e30
 
 
@@ -60,9 +61,9 @@
 
     def __call__(self, hid_in, table_in, loc_k, loc_v, glo_k, glo_v, lwq, lwk, lwv, lwo, lpre, lpost, gwq, gwk, gwv, gwo, gpre, gpost,
                  hid_out, lk_out, lv_out, gk_out, gv_out,
-                 hid_b, table, gain_b, wq_b, wk_b, wv_b, wo_b, kv_b, q_msg, q_all, p_msg, p_all, y_all,
+                 hid_b, table, gain_b, wq_b, wk_b, wv_b, wo_b, kv_b, q_msg, q_all, p_msg, p_all, y_part, y_mate, y_chip, y_half, relay_b,
                  in_sem, f_sem, g_sem, d_sem, own_sem, glo_rsem, loc_rsem, w_sem, kv_sem,
-                 qs_sem, qr_sem, ps_sem, pr_sem, ys_sem, yr_sem):
+                 qs_sem, qr_sem, ps_sem, pr_sem, m_sem, ys_sem, yr_sem, h_sem, r_sem):
         n, blk, hd = self.n, self.blk, self.hd
         half = hd // 2
         me = lax.axis_index("a")
@@ -88,8 +89,10 @@
         def glo_dst(out, src_dev):
             return out.at[0, 0, pl.ds(pl.multiple_of(src_dev * blk, blk), blk)]
 
-        def loc_dst(out, src_dev):
-            return out.at[0, 0, pl.ds(pl.multiple_of(lax.rem(src_dev * blk, WINDOW), blk), blk)]
+        def loc_dst(out, src_dev, lo=0):
+            if lo == 0:
+                return out.at[0, 0, pl.ds(pl.multiple_of(lax.rem(src_dev * blk, WINDOW), blk), blk)]
+            return out.at[0, 0, pl.ds(pl.multiple_of(lax.rem(src_dev * blk, WINDOW) + lo, 32), blk - lo)]
 
         in_cp = [pltpu.make_async_copy(hid_in, hid_b, in_sem.at[0]), pltpu.make_async_copy(table_in, table, in_sem.at[1])]
         in_cp += [pltpu.make_async_copy(g, b, in_sem.at[2 + j]) for j, (g, b) in enumerate(zip((lpre, lpost, gpre, gpost), gain_b))]
@@ -110,38 +113,64 @@
             return pltpu.make_async_remote_copy(src_ref=src.at[0, dst], dst_ref=glo_dst(out, me), send_sem=sem,
                                                 recv_sem=glo_rsem.at[kv, me], device_id={"a": dst}, device_id_type=MESH)
 
-        def loc_send(kv, dst, sem):
+        def loc_send(kv, dst, sem, lo=0):
             src, out = loc_pairs[kv]
-            return pltpu.make_async_remote_copy(src_ref=src.at[0, dst], dst_ref=loc_dst(out, me), send_sem=sem,
+            return pltpu.make_async_remote_copy(src_ref=src.at[0, dst, lo:], dst_ref=loc_dst(out, me, lo), send_sem=sem,
                                                 recv_sem=loc_rsem.at[kv, me], device_id={"a": dst}, device_id_type=MESH)
 
+        relay_from, relay_via = chips // 2, chips // 2 - 1
+        relay_to = (relay_from + chips // 2) % chips
+
+        def relay_send():
+            dst = relay_to * CORES + (CORES - 1 - core)
+            return pltpu.make_async_remote_copy(src_ref=loc_v.at[0, dst, pl.ds(0, RELAY)], dst_ref=relay_b, send_sem=r_sem.at[0],
+                                                recv_sem=r_sem.at[1], device_id={"a": relay_via * CORES + core}, device_id_type=MESH)
+
+        def relay_forward(src_core, dst_core):
+            src_dev = relay_from * CORES + src_core
+            dst_ref = lv_out.at[0, 0, pl.ds(pl.multiple_of(lax.rem(src_dev * blk, WINDOW), blk), RELAY)]
+            return pltpu.make_async_remote_copy(src_ref=relay_b, dst_ref=dst_ref, send_sem=r_sem.at[2],
+                                                recv_sem=r_sem.at[3], device_id={"a": relay_to * CORES + dst_core}, device_id_type=MESH)
+
+        steps = 8
+
         def step_items(step):
-            dst_chip = near_f if step < 4 else opp
-            part = step % 4
-            items = [(part % 2, dst_chip * CORES + lax.rem(core + part // 2, CORES), f_sem, step)]
-            if step < 4:
-                items.append((part % 2, near_g * CORES + lax.rem(core + part // 2, CORES), g_sem, step))
-            return items
+            part = step % steps // 2
+            kv, peer = part % 2, lax.rem(core + part // 2, CORES)
+            if step >= steps:
+                return kv, [(opp * CORES + peer, f_sem.at[step])]
+            return kv, [(near_f * CORES + peer, f_sem.at[step]), (near_g * CORES + peer, g_sem.at[step])]
+
+        def bulk(step, act):
+            kv, items = step_items(step)
+            if step % 2 == 0:
+                for dst, sem in items:
+                    act(glo_send(kv, dst, sem))
+            elif step == 2 * steps - 1:
+                (dst, sem), = items
+
+                @pl.when(chip == relay_from)
+                def _():
+                    act(loc_send(kv, dst, sem, RELAY))
+
+                @pl.when(jnp.logical_and(has_loc, chip != relay_from))
+                def _():
+                    act(loc_send(kv, dst, sem))
+            else:
+                @pl.when(has_loc)
+                def _():
+                    for dst, sem in items:
+                        act(loc_send(kv, dst, sem))
 
         def bulk_start(step):
-            items = step_items(step)
-            for kv, dst, sem, s in items:
-                glo_send(kv, dst, sem.at[s, 0]).start()
-
-            @pl.when(has_loc)
-            def _():
-                for kv, dst, sem, s in items:
-                    loc_send(kv, dst, sem.at[s, 1]).start()
+            bulk(step, lambda cp: cp.start())
 
         def bulk_wait(step):
-            items = step_items(step)
-            for kv, dst, sem, s in items:
-                glo_send(kv, dst, sem.at[s, 0]).wait_send()
-
-            @pl.when(has_loc)
-            def _():
-                for kv, dst, sem, s in items:
-                    loc_send(kv, dst, sem.at[s, 1]).wait_send()
+            bulk(step, lambda cp: cp.wait_send())
+
+        @pl.when(chip == relay_from)
+        def _():
+            relay_send().start()
 
         bulk_start(0)
         mate = chip * CORES + (CORES - 1 - core)
@@ -168,9 +197,19 @@
             return pltpu.make_async_remote_copy(src_ref=p_msg.at[la, dst], dst_ref=p_all.at[la, me], send_sem=ps_sem.at[la, i - 1],
                                                 recv_sem=pr_sem.at[la, me], device_id={"a": dst}, device_id_type=MESH)
 
-        def y_send(la, dst, i):
-            return pltpu.make_async_remote_copy(src_ref=y_all.at[la, me], dst_ref=y_all.at[la, me], send_sem=ys_sem.at[la, i - 1],
-                                                recv_sem=yr_sem.at[la, me], device_id={"a": dst}, device_id_type=MESH)
+        def mate_send(la):
+            return pltpu.make_async_remote_copy(src_ref=y_part.at[la, 1 - core], dst_ref=y_mate.at[la], send_sem=m_sem.at[la, 0],
+                                                recv_sem=m_sem.at[la, 1], device_id={"a": mate}, device_id_type=MESH)
+
+        def chip_copy(la, other, slot, i):
+            return pltpu.make_async_remote_copy(src_ref=y_chip.at[la, slot], dst_ref=y_chip.at[la, slot], send_sem=ys_sem.at[la, i],
+                                                recv_sem=yr_sem.at[la, slot], device_id={"a": other * CORES + core}, device_id_type=MESH)
+
+        def half_copy(la, slot):
+            return pltpu.make_async_remote_copy(src_ref=y_half.at[la, slot], dst_ref=y_half.at[la, slot], send_sem=h_sem.at[la, 0],
+                                                recv_sem=h_sem.at[la, 1], device_id={"a": mate}, device_id_type=MESH)
+
+        others = [(lax.rem(chip + i, chips), i - 1) for i in range(1, chips)]
 
         def q_arrival(la, src):
             return pltpu.make_async_remote_copy(src_ref=q_msg.at[la], dst_ref=q_all.at[la, src], send_sem=qs_sem.at[la, 0],
@@ -179,10 +218,6 @@
         def p_arrival(la, src):
             return pltpu.make_async_remote_copy(src_ref=p_msg.at[la, 0], dst_ref=p_all.at[la, src], send_sem=ps_sem.at[la, 0],
                                                 recv_sem=pr_sem.at[la, src], device_id={"a": src}, device_id_type=MESH)
-
-        def y_arrival(la, src):
-            return pltpu.make_async_remote_copy(src_ref=y_all.at[la, src], dst_ref=y_all.at[la, src], send_sem=ys_sem.at[la, 0],
-                                                recv_sem=yr_sem.at[la, src], device_id={"a": src}, device_id_type=MESH)
 
         def peers():
             return [(lax.rem(me + i, n), i) for i in range(1, n)]
@@ -281,9 +316,13 @@
                     part = jnp.dot(lhs[g], wo_b[la, g * hd:(g + 1) * hd, i * ROW:(i + 1) * ROW], preferred_element_type=jnp.float32)
                     y = part if y is None else y + part
                 msg = jnp.where(row == i, y[:8], msg)
-            y_all[la, me] = msg.astype(jnp.bfloat16)
-            for dst, i in peers():
-                y_send(la, dst, i).start()
+            y_part[la, 0] = msg[:4]
+            y_part[la, 1] = msg[4:]
+            mate_send(la).start()
+            mate_send(la).wait_recv()
+            y_chip[la, chip] = y_part[la, core] + y_mate[la]
+            for other, i in others:
+                chip_copy(la, other, chip, i).start()
 
         hidden = tiled(lambda i: hid_b[:, i * ROW:(i + 1) * ROW].astype(jnp.float32))
         fresh = []
@@ -294,20 +333,24 @@
             q_msg[la] = q
             q_all[la, me] = q
             for dst, i in peers():
-                q_send(la, dst, i).start()
+                @pl.when(jnp.logical_or(la == 1, dst >= self.first_src))
+                def _():
+                    q_send(la, dst, i).start()
             step = 3 * la + 1
             bulk_start(step)
             bulk_wait(step - 1)
             if la == 0:
                 for cp in w_cp[1] + kv_cp[1]:
                     cp.start()
-            for src, i in peers():
-                q_arrival(la, src).wait_recv()
             if la == 0:
                 @pl.when(has_loc)
                 def _():
+                    for src, i in peers():
+                        q_arrival(0, src).wait_recv()
                     attend_all(0, True)
             else:
+                for src, i in peers():
+                    q_arrival(1, src).wait_recv()
                 attend_all(1, False)
             bulk_start(step + 1)
             bulk_wait(step)
@@ -322,16 +365,27 @@
             out_project(la, combine(la, q, k_new, v_new, first_src))
             bulk_start(step + 2)
             bulk_wait(step + 1)
-            for src, i in peers():
-                y_arrival(la, src).wait_recv()
-            y = y_all[la, 0].astype(jnp.float32)
-            for s in range(1, n):
-                y = y + y_all[la, s].astype(jnp.float32)
+            for other, i in others:
+                chip_copy(la, other, other, i).wait_recv()
+            total = y_chip[la, 0]
+            for c in range(1, chips):
+                total = total + y_chip[la, c]
+            y_half[la, core] = total
+            half_copy(la, core).start()
+            half_copy(la, 1 - core).wait_recv()
+            y = jnp.concatenate([y_half[la, 0], y_half[la, 1]], axis=0)
             hidden = round_bf16(hidden + norm(y) * (1.0 + post))
         for i in range(self.chunks):
             hid_out[:, i * ROW:(i + 1) * ROW] = hidden[i:i + 1, :].astype(jnp.bfloat16)
 
-        bulk_start(7)
+        for step in range(7, 2 * steps):
+            bulk_start(step)
+
+        @pl.when(chip == relay_via)
+        def _():
+            relay_send().wait_recv()
+            relay_forward(core, CORES - 1 - core).start()
+
         row16 = lax.broadcasted_iota(jnp.int32, (16, hd), 0)
         for kv, out in enumerate((gk_out, gv_out)):
             new = jnp.broadcast_to(fresh[1][kv][0:1], (16, hd))
@@ -340,8 +394,13 @@
 
         for la in range(2):
             for dst, i in peers():
-                q_send(la, dst, i).wait_send()
-                y_send(la, dst, i).wait_send()
+                @pl.when(jnp.logical_or(la == 1, dst >= self.first_src))
+                def _():
+                    q_send(la, dst, i).wait_send()
+            mate_send(la).wait_send()
+            for other, i in others:
+                chip_copy(la, other, chip, i).wait_send()
+            half_copy(la, core).wait_send()
         for dst, i in peers():
             p_send(1, dst, i).wait_send()
 
@@ -362,24 +421,46 @@
             return pltpu.make_async_remote_copy(src_ref=src.at[0, 0], dst_ref=glo_dst(out, src_dev), send_sem=d_sem.at[0, kv],
                                                 recv_sem=glo_rsem.at[kv, src_dev], device_id={"a": src_dev}, device_id_type=MESH)
 
-        def loc_arrival(kv, src_dev):
+        def loc_arrival(kv, src_dev, lo=0):
             src, out = loc_pairs[kv]
-            return pltpu.make_async_remote_copy(src_ref=src.at[0, 0], dst_ref=loc_dst(out, src_dev), send_sem=d_sem.at[1, kv],
+            return pltpu.make_async_remote_copy(src_ref=src.at[0, 0, lo:], dst_ref=loc_dst(out, src_dev, lo), send_sem=d_sem.at[1, kv],
                                                 recv_sem=loc_rsem.at[kv, src_dev], device_id={"a": src_dev}, device_id_type=MESH)
 
         for src_dev, i in peers():
+            short = jnp.logical_and(chip == relay_to, src_dev == relay_from * CORES + (CORES - 1 - core))
+
             @pl.when(src_dev >= self.first_src)
             def _():
-                for kv in range(2):
-                    loc_arrival(kv, src_dev).wait_recv()
+                loc_arrival(0, src_dev).wait_recv()
+
+            @pl.when(jnp.logical_and(src_dev >= self.first_src, jnp.logical_not(short)))
+            def _():
+                loc_arrival(1, src_dev).wait_recv()
+
+            @pl.when(short)
+            def _():
+                loc_arrival(1, src_dev, RELAY).wait_recv()
+
+        @pl.when(chip == relay_from)
+        def _():
+            relay_send().wait_send()
+
+        @pl.when(chip == relay_via)
+        def _():
+            relay_forward(core, CORES - 1 - core).wait_send()
+
+        @pl.when(chip == relay_to)
+        def _():
+            relay_forward(CORES - 1 - core, core).wait_recv()
+
         slot = (self.seq % WINDOW) // 16 * 16
         for kv, out in enumerate((lk_out, lv_out)):
             new = jnp.broadcast_to(fresh[0][kv][0:1], (16, hd))
             old = out[0, 0, slot:slot + 16, :].astype(jnp.float32)
             out[0, 0, slot:slot + 16, :] = jnp.where(row16 == self.seq % WINDOW - slot, new, old).astype(jnp.bfloat16)
 
-        bulk_wait(6)
-        bulk_wait(7)
+        for step in range(6, 2 * steps):
+            bulk_wait(step)
         for src_dev, i in peers():
             for kv in range(2):
                 glo_arrival(kv, src_dev).wait_recv()
@@ -431,9 +512,13 @@
                 pltpu.VMEM((2, n, 2, hd), f32),
                 pltpu.VMEM((2, n, 2, hd + 128), f32),
                 pltpu.VMEM((2, n, 2, hd + 128), f32),
-                pltpu.VMEM((2, n, 8, ROW), bf16),
-                dma((6,)), dma((8, 2)), dma((4, 2)), dma((2, 2)), dma((2, 2)), dma((2, n)), dma((2, n)), dma((2, 4)), dma((2, 2)),
-                dma((2, n - 1)), dma((2, n)), dma((2, n - 1)), dma((2, n)), dma((2, n - 1)), dma((2, n)),
+                pltpu.VMEM((2, CORES, 4, ROW), f32),
+                pltpu.VMEM((2, 4, ROW), f32),
+                pltpu.VMEM((2, n // CORES, 4, ROW), f32),
+                pltpu.VMEM((2, CORES, 4, ROW), f32),
+                pltpu.VMEM((RELAY, hd), bf16),
+                dma((6,)), dma((16,)), dma((8,)), dma((2, 2)), dma((2, 2)), dma((2, n)), dma((2, n)), dma((2, 4)), dma((2, 2)),
+                dma((2, n - 1)), dma((2, n)), dma((2, n - 1)), dma((2, n)), dma((2, 2)), dma((2, 3)), dma((2, n // CORES)), dma((2, 2)), dma((4,)),
             ],
             compiler_params=pltpu.CompilerParams(collective_id=0, has_side_effects=True, vmem_limit_bytes=48 * 2**20),
         )(hidden_in, table, loc_k, loc_v, glo_k, glo_v, loc_wq, loc_wk, loc_wv, loc_wo, loc_pre, loc_post, glo_wq, glo_wk, glo_wv, glo_wo, glo_pre, glo_post)

time: 196 us -> 194 us (0.990)
  Pallas kernels: 195 us -> 193 us
    pallas_call x1, Pallas kernels: 191 us -> 189 us  [device_step(): pl.pallas_call(Kernel(n, d_model, heads, blk, hd, slots), name='decode_st...]
where the time goes in v3:
time: 194 us
  Pallas kernels  193 us (99%)
    pallas_call x1, Pallas kernels, device_step(): pl.pallas_call(Kernel(n, d_model, heads, blk, hd, slots), name='decode_st...  189 us
    pallas_call x1, Pallas kernels, device_step(): pl.pallas_call(store_outputs, name='store_outputs', out_shape=tuple((jax....  4.85 us

profile of v3, /device:TPU:81, one launch (start us, length us, event | category | flops | bytes accessed | tf_op | source)
XLA Modules:
  0.0 194.0 jit_solution(9011785142754902187)
XLA Ops:
  0.6 188.5 %decode_step.1 = (bf16[1,3584]{1,0:T(2,128)(2,1)S(1)}, bf16[1,1,4096,256]{3,2,1,0:T(8,128)(2,1)S(1)}, bf16[1,1,4096,256]{3,2,1,0:T(8,128)(2,1)S(1)}, bf16[1,1,87...) custom-call(bf16[1,3584]{1,0:T(2,128)(2,1)} %hid_in.1, f32[2,128]{1,0:T(2,128)} %constant.2.clone.table_in, ...), custom_call_target="tpu_custom_call" | custom-call | tf_op jit(solution)/shard_map/decode_step/pallas_call | solution.py:490
  189.2 4.8 %store_outputs.1 = (bf16[1,3584]{1,0:T(2,128)(2,1)}, bf16[1,1,4096,256]{3,2,1,0:T(8,128)(2,1)}, bf16[1,1,4096,256]{3,2,1,0:T(8,128)(2,1)}, bf16[1,1,8704,256]{3,2,1,0:T(8,128)(2,1)}, bf16[1,1,8704,256]{3,2,1,0:T(8,128)(2,1)}) custom-call(bf16[1,3584]{1,0:T(2,128)(2,1)S(1)} %get-tuple-element.10.refs_0_, ...), custom_call_target="tpu_custom_call" | custom-call | tf_op jit(solution)/shard_map/store_outputs/pallas_call | solution.py:525

commit v4 on v3

--- a/solution.py
+++ b/solution.py
@@ -17,7 +17,8 @@
 CORES = 2
 ROW = 512
 STORE_PARTS = 2
-RELAY = 96
+RELAY = 128
+HOLD = 1
 NEG = -1e30
 
 
@@ -63,7 +64,7 @@
                  hid_out, lk_out, lv_out, gk_out, gv_out,
                  hid_b, table, gain_b, wq_b, wk_b, wv_b, wo_b, kv_b, q_msg, q_all, p_msg, p_all, y_part, y_mate, y_chip, y_half, relay_b,
                  in_sem, f_sem, g_sem, d_sem, own_sem, glo_rsem, loc_rsem, w_sem, kv_sem,
-                 qs_sem, qr_sem, ps_sem, pr_sem, m_sem, ys_sem, yr_sem, h_sem, r_sem):
+                 qs_sem, qr_sem, ps_sem, pr_sem, m_sem, ys_sem, yr_sem, h_sem, r_sem, go_sem):
         n, blk, hd = self.n, self.blk, self.hd
         half = hd // 2
         me = lax.axis_index("a")
@@ -75,9 +76,33 @@
         near_f = jnp.where(even, right, left)
         near_g = jnp.where(even, left, right)
 
+        mate = chip * CORES + (CORES - 1 - core)
+
+        relay_from, relay_via = chips // 2, chips // 2 - 1
+        relay_to = (relay_from + chips // 2) % chips
+
         barrier = pltpu.get_barrier_semaphore()
-        for i in range(1, n):
-            pl.semaphore_signal(barrier, inc=1, device_id={"a": lax.rem(me + i, n)}, device_id_type=MESH)
+
+        def greet(devices):
+            for dev in devices:
+                pl.semaphore_signal(barrier, inc=1, device_id={"a": dev}, device_id_type=MESH)
+
+        def cores_of(c):
+            return [c * CORES + j for j in range(CORES)]
+
+        def tell(c):
+            pl.semaphore_signal(go_sem, inc=1, device_id={"a": c * CORES + core}, device_id_type=MESH)
+
+        late = chips - 1
+        early_devices = list(range(self.first_src))
+
+        @pl.when(jnp.logical_not(has_loc))
+        def _():
+            greet([mate] + cores_of(near_f) + cores_of(near_g))
+
+        @pl.when(chip == late)
+        def _():
+            greet([mate] + early_devices)
 
         weights = [((lwq, gwq), wq_b), ((lwk, gwk), wk_b), ((lwv, gwv), wv_b), ((lwo, gwo), wo_b)]
         w_cp = [[pltpu.make_async_copy(srcs[la], dst.at[la], w_sem.at[la, j]) for j, (srcs, dst) in enumerate(weights)] for la in range(2)]
@@ -92,7 +117,7 @@
         def loc_dst(out, src_dev, lo=0):
             if lo == 0:
                 return out.at[0, 0, pl.ds(pl.multiple_of(lax.rem(src_dev * blk, WINDOW), blk), blk)]
-            return out.at[0, 0, pl.ds(pl.multiple_of(lax.rem(src_dev * blk, WINDOW) + lo, 32), blk - lo)]
+            return out.at[0, 0, pl.ds(pl.multiple_of(lax.rem(src_dev * blk, WINDOW) + lo, 16), blk - lo)]
 
         in_cp = [pltpu.make_async_copy(hid_in, hid_b, in_sem.at[0]), pltpu.make_async_copy(table_in, table, in_sem.at[1])]
         in_cp += [pltpu.make_async_copy(g, b, in_sem.at[2 + j]) for j, (g, b) in enumerate(zip((lpre, lpost, gpre, gpost), gain_b))]
@@ -106,7 +131,14 @@
 
         w_cp[0][3].start()
 
-        pl.semaphore_wait(barrier, n - 1)
+        @pl.when(jnp.logical_not(has_loc))
+        def _():
+            pl.semaphore_wait(barrier, n - 1)
+
+        @pl.when(chip == late)
+        def _():
+            pl.semaphore_wait(barrier, 1 + 2 * CORES)
+            tell(relay_from)
 
         def glo_send(kv, dst, sem):
             src, out = glo_pairs[kv]
@@ -117,9 +149,6 @@
             src, out = loc_pairs[kv]
             return pltpu.make_async_remote_copy(src_ref=src.at[0, dst, lo:], dst_ref=loc_dst(out, me, lo), send_sem=sem,
                                                 recv_sem=loc_rsem.at[kv, me], device_id={"a": dst}, device_id_type=MESH)
-
-        relay_from, relay_via = chips // 2, chips // 2 - 1
-        relay_to = (relay_from + chips // 2) % chips
 
         def relay_send():
             dst = relay_to * CORES + (CORES - 1 - core)
@@ -135,18 +164,19 @@
         steps = 8
 
         def step_items(step):
-            part = step % steps // 2
+            part = step // 2 if step < steps else step % 4
             kv, peer = part % 2, lax.rem(core + part // 2, CORES)
             if step >= steps:
                 return kv, [(opp * CORES + peer, f_sem.at[step])]
             return kv, [(near_f * CORES + peer, f_sem.at[step]), (near_g * CORES + peer, g_sem.at[step])]
 
-        def bulk(step, act):
+        def bulk(step, act, sides=slice(None)):
             kv, items = step_items(step)
-            if step % 2 == 0:
+            items = items[sides]
+            if step >= 12 or (step < steps and step % 2 == 0):
                 for dst, sem in items:
                     act(glo_send(kv, dst, sem))
-            elif step == 2 * steps - 1:
+            elif step == 11:
                 (dst, sem), = items
 
                 @pl.when(chip == relay_from)
@@ -162,18 +192,25 @@
                     for dst, sem in items:
                         act(loc_send(kv, dst, sem))
 
-        def bulk_start(step):
-            bulk(step, lambda cp: cp.start())
+        def bulk_start(step, sides=slice(None)):
+            bulk(step, lambda cp: cp.start(), sides)
 
         def bulk_wait(step):
             bulk(step, lambda cp: cp.wait_send())
 
         @pl.when(chip == relay_from)
         def _():
+            pl.semaphore_wait(barrier, CORES)
+            greet(early_devices + cores_of(late))
             relay_send().start()
-
-        bulk_start(0)
-        mate = chip * CORES + (CORES - 1 - core)
+            bulk_start(0, slice(1, 2))
+            pl.semaphore_wait(go_sem, 1)
+            bulk_start(0, slice(0, 1))
+
+        @pl.when(chip != relay_from)
+        def _():
+            bulk_start(0)
+
         own_glo = [pltpu.make_async_copy(src.at[0, me], glo_dst(out, me), own_sem.at[0, kv]) for kv, (src, out) in enumerate(glo_pairs)]
         own_loc = [pltpu.make_async_copy(src.at[0, me], loc_dst(out, me), own_sem.at[1, kv]) for kv, (src, out) in enumerate(loc_pairs)]
         for kv in range(2):
@@ -363,8 +400,24 @@
                 else:
                     p_arrival(la, src).wait_recv()
             out_project(la, combine(la, q, k_new, v_new, first_src))
-            bulk_start(step + 2)
-            bulk_wait(step + 1)
+            if la == 0:
+                bulk_start(step + 2)
+                bulk_wait(step + 1)
+            else:
+                for later in range(step + 2, steps - HOLD):
+                    bulk_start(later)
+                for later in range(steps - HOLD, steps):
+                    bulk_start(later, slice(1, 2))
+                for later in range(steps, 2 * steps):
+                    bulk_start(later)
+                for later in range(steps - HOLD, steps):
+                    bulk_start(later, slice(0, 1))
+
+                @pl.when(chip == relay_via)
+                def _():
+                    relay_send().wait_recv()
+                    relay_forward(core, CORES - 1 - core).start()
+
             for other, i in others:
                 chip_copy(la, other, other, i).wait_recv()
             total = y_chip[la, 0]
@@ -378,14 +431,6 @@
         for i in range(self.chunks):
             hid_out[:, i * ROW:(i + 1) * ROW] = hidden[i:i + 1, :].astype(jnp.bfloat16)
 
-        for step in range(7, 2 * steps):
-            bulk_start(step)
-
-        @pl.when(chip == relay_via)
-        def _():
-            relay_send().wait_recv()
-            relay_forward(core, CORES - 1 - core).start()
-
         row16 = lax.broadcasted_iota(jnp.int32, (16, hd), 0)
         for kv, out in enumerate((gk_out, gv_out)):
             new = jnp.broadcast_to(fresh[1][kv][0:1], (16, hd))
@@ -459,7 +504,7 @@
             old = out[0, 0, slot:slot + 16, :].astype(jnp.float32)
             out[0, 0, slot:slot + 16, :] = jnp.where(row16 == self.seq % WINDOW - slot, new, old).astype(jnp.bfloat16)
 
-        for step in range(6, 2 * steps):
+        for step in range(5, 2 * steps):
             bulk_wait(step)
         for src_dev, i in peers():
             for kv in range(2):
@@ -518,7 +563,7 @@
                 pltpu.VMEM((2, CORES, 4, ROW), f32),
                 pltpu.VMEM((RELAY, hd), bf16),
                 dma((6,)), dma((16,)), dma((8,)), dma((2, 2)), dma((2, 2)), dma((2, n)), dma((2, n)), dma((2, 4)), dma((2, 2)),
-                dma((2, n - 1)), dma((2, n)), dma((2, n - 1)), dma((2, n)), dma((2, 2)), dma((2, 3)), dma((2, n // CORES)), dma((2, 2)), dma((4,)),
+                dma((2, n - 1)), dma((2, n)), dma((2, n - 1)), dma((2, n)), dma((2, 2)), dma((2, 3)), dma((2, n // CORES)), dma((2, 2)), dma((4,)), pltpu.SemaphoreType.REGULAR,
             ],
             compiler_params=pltpu.CompilerParams(collective_id=0, has_side_effects=True, vmem_limit_bytes=48 * 2**20),
         )(hidden_in, table, loc_k, loc_v, glo_k, glo_v, loc_wq, loc_wk, loc_wv, loc_wo, loc_pre, loc_post, glo_wq, glo_wk, glo_wv, glo_wo, glo_pre, glo_post)

time: 194 us -> 193 us (level)
  no operation moved by 1% of the time
where the time goes in v4:
time: 193 us
  Pallas kernels  192 us (99%)
    pallas_call x1, Pallas kernels, device_step(): pl.pallas_call(Kernel(n, d_model, heads, blk, hd, slots), name='decode_st...  187 us
    pallas_call x1, Pallas kernels, device_step(): pl.pallas_call(store_outputs, name='store_outputs', out_shape=tuple((jax....  4.85 us

profile of v4, /device:TPU:81, one launch (start us, length us, event | category | flops | bytes accessed | tf_op | source)
XLA Modules:
  0.0 192.9 jit_solution(11461209174092112674)
XLA Ops:
  0.6 187.4 %decode_step.1 = (bf16[1,3584]{1,0:T(2,128)(2,1)S(1)}, bf16[1,1,4096,256]{3,2,1,0:T(8,128)(2,1)S(1)}, bf16[1,1,4096,256]{3,2,1,0:T(8,128)(2,1)S(1)}, bf16[1,1,87...) custom-call(bf16[1,3584]{1,0:T(2,128)(2,1)} %hid_in.1, f32[2,128]{1,0:T(2,128)} %constant.2.clone.table_in, ...), custom_call_target="tpu_custom_call" | custom-call | tf_op jit(solution)/shard_map/decode_step/pallas_call | solution.py:535
  188.1 4.8 %store_outputs.1 = (bf16[1,3584]{1,0:T(2,128)(2,1)}, bf16[1,1,4096,256]{3,2,1,0:T(8,128)(2,1)}, bf16[1,1,4096,256]{3,2,1,0:T(8,128)(2,1)}, bf16[1,1,8704,256]{3,2,1,0:T(8,128)(2,1)}, bf16[1,1,8704,256]{3,2,1,0:T(8,128)(2,1)}) custom-call(bf16[1,3584]{1,0:T(2,128)(2,1)S(1)} %get-tuple-element.10.refs_0_, ...), custom_call_target="tpu_custom_call" | custom-call | tf_op jit(solution)/shard_map/store_outputs/pallas_call | solution.py:570

commit v5 on v4

--- a/solution.py
+++ b/solution.py
@@ -17,8 +17,9 @@
 CORES = 2
 ROW = 512
 STORE_PARTS = 2
-RELAY = 128
+RELAY = 112
 HOLD = 1
+SCHEDULE = (1, 2, 3, 4, 5, 6)
 NEG = -1e30
 
 
@@ -104,6 +105,10 @@
         def _():
             greet([mate] + early_devices)
 
+        @pl.when(chip == relay_from)
+        def _():
+            greet(cores_of(late) + early_devices)
+
         weights = [((lwq, gwq), wq_b), ((lwk, gwk), wk_b), ((lwv, gwv), wv_b), ((lwo, gwo), wo_b)]
         w_cp = [[pltpu.make_async_copy(srcs[la], dst.at[la], w_sem.at[la, j]) for j, (srcs, dst) in enumerate(weights)] for la in range(2)]
         kv_cp = [[pltpu.make_async_copy(src.at[0], kv_b.at[la, j], kv_sem.at[la, j]) for j, src in enumerate(pair)]
@@ -201,10 +206,10 @@
         @pl.when(chip == relay_from)
         def _():
             pl.semaphore_wait(barrier, CORES)
-            greet(early_devices + cores_of(late))
             relay_send().start()
             bulk_start(0, slice(1, 2))
             pl.semaphore_wait(go_sem, 1)
+            tell(late)
             bulk_start(0, slice(0, 1))
 
         @pl.when(chip != relay_from)
@@ -361,6 +366,12 @@
             for other, i in others:
                 chip_copy(la, other, chip, i).start()
 
+        def stage(k):
+            for step in range(SCHEDULE[k], SCHEDULE[k + 1]):
+                bulk_start(step)
+            for step in range(SCHEDULE[k - 1] if k else 0, SCHEDULE[k]):
+                bulk_wait(step)
+
         hidden = tiled(lambda i: hid_b[:, i * ROW:(i + 1) * ROW].astype(jnp.float32))
         fresh = []
         for la in range(2):
@@ -373,15 +384,17 @@
                 @pl.when(jnp.logical_or(la == 1, dst >= self.first_src))
                 def _():
                     q_send(la, dst, i).start()
-            step = 3 * la + 1
-            bulk_start(step)
-            bulk_wait(step - 1)
+            stage(3 * la)
             if la == 0:
                 for cp in w_cp[1] + kv_cp[1]:
                     cp.start()
             if la == 0:
                 @pl.when(has_loc)
                 def _():
+                    @pl.when(chip == late)
+                    def _():
+                        pl.semaphore_wait(go_sem, 1)
+
                     for src, i in peers():
                         q_arrival(0, src).wait_recv()
                     attend_all(0, True)
@@ -389,8 +402,7 @@
                 for src, i in peers():
                     q_arrival(1, src).wait_recv()
                 attend_all(1, False)
-            bulk_start(step + 1)
-            bulk_wait(step)
+            stage(3 * la + 1)
             first_src = self.first_src if la == 0 else 0
             for src, i in peers():
                 if la == 0:
@@ -401,10 +413,9 @@
                     p_arrival(la, src).wait_recv()
             out_project(la, combine(la, q, k_new, v_new, first_src))
             if la == 0:
-                bulk_start(step + 2)
-                bulk_wait(step + 1)
+                stage(2)
             else:
-                for later in range(step + 2, steps - HOLD):
+                for later in range(SCHEDULE[5], steps - HOLD):
                     bulk_start(later)
                 for later in range(steps - HOLD, steps):
                     bulk_start(later, slice(1, 2))
@@ -504,7 +515,7 @@
             old = out[0, 0, slot:slot + 16, :].astype(jnp.float32)
             out[0, 0, slot:slot + 16, :] = jnp.where(row16 == self.seq % WINDOW - slot, new, old).astype(jnp.bfloat16)
 
-        for step in range(5, 2 * steps):
+        for step in range(SCHEDULE[4], 2 * steps):
             bulk_wait(step)
         for src_dev, i in peers():
             for kv in range(2):

time: 193 us -> 193 us (level)
  no operation moved by 1% of the time
where the time goes in v5:
time: 193 us
  Pallas kernels  192 us (99%)
    pallas_call x1, Pallas kernels, device_step(): pl.pallas_call(Kernel(n, d_model, heads, blk, hd, slots), name='decode_st...  187 us
    pallas_call x1, Pallas kernels, device_step(): pl.pallas_call(store_outputs, name='store_outputs', out_shape=tuple((jax....  4.85 us

profile of v5, /device:TPU:81, one launch (start us, length us, event | category | flops | bytes accessed | tf_op | source)
XLA Modules:
  0.0 192.7 jit_solution(5760343374755571396)
XLA Ops:
  0.6 187.2 %decode_step.1 = (bf16[1,3584]{1,0:T(2,128)(2,1)S(1)}, bf16[1,1,4096,256]{3,2,1,0:T(8,128)(2,1)S(1)}, bf16[1,1,4096,256]{3,2,1,0:T(8,128)(2,1)S(1)}, bf16[1,1,87...) custom-call(bf16[1,3584]{1,0:T(2,128)(2,1)} %hid_in.1, f32[2,128]{1,0:T(2,128)} %constant.2.clone.table_in, ...), custom_call_target="tpu_custom_call" | custom-call | tf_op jit(solution)/shard_map/decode_step/pallas_call | solution.py:546
  187.8 4.8 %store_outputs.1 = (bf16[1,3584]{1,0:T(2,128)(2,1)}, bf16[1,1,4096,256]{3,2,1,0:T(8,128)(2,1)}, bf16[1,1,4096,256]{3,2,1,0:T(8,128)(2,1)}, bf16[1,1,8704,256]{3,2,1,0:T(8,128)(2,1)}, bf16[1,1,8704,256]{3,2,1,0:T(8,128)(2,1)}) custom-call(bf16[1,3584]{1,0:T(2,128)(2,1)S(1)} %get-tuple-element.10.refs_0_, ...), custom_call_target="tpu_custom_call" | custom-call | tf_op jit(solution)/shard_map/store_outputs/pallas_call | solution.py:581

commit v6 on v5

--- a/solution.py
+++ b/solution.py
@@ -63,9 +63,9 @@
 
     def __call__(self, hid_in, table_in, loc_k, loc_v, glo_k, glo_v, lwq, lwk, lwv, lwo, lpre, lpost, gwq, gwk, gwv, gwo, gpre, gpost,
                  hid_out, lk_out, lv_out, gk_out, gv_out,
-                 hid_b, table, gain_b, wq_b, wk_b, wv_b, wo_b, kv_b, q_msg, q_all, p_msg, p_all, y_part, y_mate, y_chip, y_half, relay_b,
+                 hid_b, table, gain_b, wq_b, wk_b, wv_b, wo_b, kv_b, q_msg, q_all, p_msg, p_mate, p_out, p_all, y_part, y_mate, y_chip, y_half, relay_b,
                  in_sem, f_sem, g_sem, d_sem, own_sem, glo_rsem, loc_rsem, w_sem, kv_sem,
-                 qs_sem, qr_sem, ps_sem, pr_sem, m_sem, ys_sem, yr_sem, h_sem, r_sem, go_sem):
+                 qs_sem, qr_sem, pm_sem, ps_sem, pr_sem, m_sem, ys_sem, yr_sem, h_sem, r_sem, go_sem):
         n, blk, hd = self.n, self.blk, self.hd
         half = hd // 2
         me = lax.axis_index("a")
@@ -178,7 +178,7 @@
         def bulk(step, act, sides=slice(None)):
             kv, items = step_items(step)
             items = items[sides]
-            if step >= 12 or (step < steps and step % 2 == 0):
+            if step >= 12 or (step < steps and step % 2 == 1):
                 for dst, sem in items:
                     act(glo_send(kv, dst, sem))
             elif step == 11:
@@ -235,9 +235,13 @@
             return pltpu.make_async_remote_copy(src_ref=q_msg.at[la], dst_ref=q_all.at[la, me], send_sem=qs_sem.at[la, i - 1],
                                                 recv_sem=qr_sem.at[la, me], device_id={"a": dst}, device_id_type=MESH)
 
-        def p_send(la, dst, i):
-            return pltpu.make_async_remote_copy(src_ref=p_msg.at[la, dst], dst_ref=p_all.at[la, me], send_sem=ps_sem.at[la, i - 1],
-                                                recv_sem=pr_sem.at[la, me], device_id={"a": dst}, device_id_type=MESH)
+        def p_mate_send(la):
+            return pltpu.make_async_remote_copy(src_ref=p_msg.at[la, 1 - core], dst_ref=p_mate.at[la], send_sem=pm_sem.at[la, 0],
+                                                recv_sem=pm_sem.at[la, 1], device_id={"a": mate}, device_id_type=MESH)
+
+        def p_send(la, other, i):
+            return pltpu.make_async_remote_copy(src_ref=p_out.at[la, other], dst_ref=p_all.at[la, chip], send_sem=ps_sem.at[la, i],
+                                                recv_sem=pr_sem.at[la, chip], device_id={"a": other * CORES + core}, device_id_type=MESH)
 
         def mate_send(la):
             return pltpu.make_async_remote_copy(src_ref=y_part.at[la, 1 - core], dst_ref=y_mate.at[la], send_sem=m_sem.at[la, 0],
@@ -257,9 +261,9 @@
             return pltpu.make_async_remote_copy(src_ref=q_msg.at[la], dst_ref=q_all.at[la, src], send_sem=qs_sem.at[la, 0],
                                                 recv_sem=qr_sem.at[la, src], device_id={"a": src}, device_id_type=MESH)
 
-        def p_arrival(la, src):
-            return pltpu.make_async_remote_copy(src_ref=p_msg.at[la, 0], dst_ref=p_all.at[la, src], send_sem=ps_sem.at[la, 0],
-                                                recv_sem=pr_sem.at[la, src], device_id={"a": src}, device_id_type=MESH)
+        def p_arrival(la, other):
+            return pltpu.make_async_remote_copy(src_ref=p_out.at[la, other], dst_ref=p_all.at[la, other], send_sem=ps_sem.at[la, 0],
+                                                recv_sem=pr_sem.at[la, other], device_id={"a": other * CORES + core}, device_id_type=MESH)
 
         def peers():
             return [(lax.rem(me + i, n), i) for i in range(1, n)]
@@ -302,7 +306,7 @@
             return q, round_bf16(rope(k)), round_bf16(v)
 
         def attend_block(la, h, masked):
-            q = q_all[la, h].astype(jnp.bfloat16)
+            q = q_all[la, h]
             s = lax.dot_general(q, kv_b[la, 0, h], (((1,), (1,)), ((), ())), preferred_element_type=jnp.float32)
             s = softcap(s, hd ** -0.5)
             if masked:
@@ -315,8 +319,8 @@
             total = jnp.sum(e, axis=1, keepdims=True)
             o = jnp.dot(e.astype(jnp.bfloat16), kv_b[la, 1, h], preferred_element_type=jnp.float32)
             lane = lax.broadcasted_iota(jnp.int32, (2, 128), 1)
-            p_msg[la, h, :, 0:hd] = o
-            p_msg[la, h, :, hd:hd + 128] = jnp.where(lane < 64, top, total)
+            p_msg[la, lax.rem(h, CORES), h // CORES, :, 0:hd] = o
+            p_msg[la, lax.rem(h, CORES), h // CORES, :, hd:hd + 128] = jnp.where(lane < 64, top, total)
 
         def attend_all(la, masked):
             for cp in kv_cp[la]:
@@ -327,25 +331,30 @@
                 return carry
 
             lax.fori_loop(0, n, body, 0)
-            for dst, i in peers():
-                p_send(la, dst, i).start()
-            p_all[la, me] = p_msg[la, me]
-
-        def combine(la, q, k_new, v_new, first_src):
+            p_mate_send(la).start()
+            p_mate_send(la).wait_recv()
+            lane = lax.broadcasted_iota(jnp.int32, (2, 128), 1)
+            for c in range(chips):
+                top, total, o = merge([p_msg[la, core, c], p_mate[la, c]])
+                p_out[la, c, :, 0:hd] = o
+                p_out[la, c, :, hd:hd + 128] = jnp.where(lane < 64, top, total)
+            for other, i in others:
+                p_send(la, other, i).start()
+            p_all[la, chip] = p_out[la, chip]
+
+        def merge(parts):
+            tops = [p[:, hd:hd + 1] for p in parts]
+            top = functools.reduce(jnp.maximum, tops)
+            weights = [jnp.exp(t - top) for t in tops]
+            total = sum(w * p[:, hd + 64:hd + 65] for w, p in zip(weights, parts))
+            return top, total, sum(w * p[:, 0:hd] for w, p in zip(weights, parts))
+
+        def combine(la, q, k_new, v_new, first_chip):
             s_new = softcap(jnp.sum(q * k_new, axis=1, keepdims=True), hd ** -0.5)
-            tops = [p_all[la, s, :, hd:hd + 1] for s in range(first_src, n)]
-            sums = [p_all[la, s, :, hd + 64:hd + 65] for s in range(first_src, n)]
-            top = s_new
-            for t in tops:
-                top = jnp.maximum(top, t)
-            e_new = jnp.exp(s_new - top)
-            denom = e_new
-            o = round_bf16(e_new) * v_new
-            for idx, s in enumerate(range(first_src, n)):
-                w = jnp.exp(tops[idx] - top)
-                denom = denom + w * sums[idx]
-                o = o + w * p_all[la, s, :, 0:hd]
-            return o / denom
+            old_top, old_total, old_o = merge([p_all[la, c] for c in range(first_chip, chips)])
+            top = jnp.maximum(s_new, old_top)
+            e_new, w = jnp.exp(s_new - top), jnp.exp(old_top - top)
+            return (round_bf16(e_new) * v_new + w * old_o) / (e_new + w * old_total)
 
         def out_project(la, o):
             w_cp[la][3].wait()
@@ -378,8 +387,8 @@
             pre, post = gain(2 * la), gain(2 * la + 1)
             q, k_new, v_new = project(la, hidden, pre)
             fresh.append((k_new, v_new))
-            q_msg[la] = q
-            q_all[la, me] = q
+            q_msg[la] = q.astype(jnp.bfloat16)
+            q_all[la, me] = q.astype(jnp.bfloat16)
             for dst, i in peers():
                 @pl.when(jnp.logical_or(la == 1, dst >= self.first_src))
                 def _():
@@ -403,15 +412,12 @@
                     q_arrival(1, src).wait_recv()
                 attend_all(1, False)
             stage(3 * la + 1)
-            first_src = self.first_src if la == 0 else 0
-            for src, i in peers():
-                if la == 0:
-                    @pl.when(src >= first_src)
-                    def _():
-                        p_arrival(0, src).wait_recv()
-                else:
-                    p_arrival(la, src).wait_recv()
-            out_project(la, combine(la, q, k_new, v_new, first_src))
+            first_chip = self.first_src // CORES if la == 0 else 0
+            for other, i in others:
+                @pl.when(other >= first_chip)
+                def _():
+                    p_arrival(la, other).wait_recv()
+            out_project(la, combine(la, q, k_new, v_new, first_chip))
             if la == 0:
                 stage(2)
             else:
@@ -457,13 +463,15 @@
             for other, i in others:
                 chip_copy(la, other, chip, i).wait_send()
             half_copy(la, core).wait_send()
-        for dst, i in peers():
-            p_send(1, dst, i).wait_send()
+        p_mate_send(1).wait_send()
+        for other, i in others:
+            p_send(1, other, i).wait_send()
 
         @pl.when(has_loc)
         def _():
-            for dst, i in peers():
-                p_send(0, dst, i).wait_send()
+            p_mate_send(0).wait_send()
+            for other, i in others:
+                p_send(0, other, i).wait_send()
             for kv in range(2):
                 loc_send(kv, mate, d_sem.at[1, kv]).wait_send()
                 own_loc[kv].wait()
@@ -517,9 +525,10 @@
 
         for step in range(SCHEDULE[4], 2 * steps):
             bulk_wait(step)
-        for src_dev, i in peers():
-            for kv in range(2):
-                glo_arrival(kv, src_dev).wait_recv()
+        for c in (chip, near_f, opp, near_g):
+            for src_dev in ([mate] if c is chip else cores_of(c)):
+                for kv in range(2):
+                    glo_arrival(kv, src_dev).wait_recv()
 
 
 def solution(mesh):
@@ -564,17 +573,19 @@
                 pltpu.VMEM((2, d_model, kv_cols), bf16),
                 pltpu.VMEM((2, q_cols, d_model), bf16),
                 pltpu.VMEM((2, 2, heads, blk, hd), bf16),
-                pltpu.VMEM((2, 2, hd), f32),
-                pltpu.VMEM((2, n, 2, hd), f32),
-                pltpu.VMEM((2, n, 2, hd + 128), f32),
-                pltpu.VMEM((2, n, 2, hd + 128), f32),
+                pltpu.VMEM((2, 2, hd), bf16),
+                pltpu.VMEM((2, n, 2, hd), bf16),
+                pltpu.VMEM((2, CORES, n // CORES, 2, hd + 128), f32),
+                pltpu.VMEM((2, n // CORES, 2, hd + 128), f32),
+                pltpu.VMEM((2, n // CORES, 2, hd + 128), f32),
+                pltpu.VMEM((2, n // CORES, 2, hd + 128), f32),
                 pltpu.VMEM((2, CORES, 4, ROW), f32),
                 pltpu.VMEM((2, 4, ROW), f32),
                 pltpu.VMEM((2, n // CORES, 4, ROW), f32),
                 pltpu.VMEM((2, CORES, 4, ROW), f32),
                 pltpu.VMEM((RELAY, hd), bf16),
                 dma((6,)), dma((16,)), dma((8,)), dma((2, 2)), dma((2, 2)), dma((2, n)), dma((2, n)), dma((2, 4)), dma((2, 2)),
-                dma((2, n - 1)), dma((2, n)), dma((2, n - 1)), dma((2, n)), dma((2, 2)), dma((2, 3)), dma((2, n // CORES)), dma((2, 2)), dma((4,)), pltpu.SemaphoreType.REGULAR,
+                dma((2, n - 1)), dma((2, n)), dma((2, 2)), dma((2, 3)), dma((2, n // CORES)), dma((2, 2)), dma((2, 3)), dma((2, n // CORES)), dma((2, 2)), dma((4,)), pltpu.SemaphoreType.REGULAR,
             ],
             compiler_params=pltpu.CompilerParams(collective_id=0, has_side_effects=True, vmem_limit_bytes=48 * 2**20),
         )(hidden_in, table, loc_k, loc_v, glo_k, glo_v, loc_wq, loc_wk, loc_wv, loc_wo, loc_pre, loc_post, glo_wq, glo_wk, glo_wv, glo_wo, glo_pre, glo_post)

time: 193 us -> 192 us (level)
  no operation moved by 1% of the time
where the time goes in v6:
time: 192 us
  Pallas kernels  192 us (100%)
    pallas_call x1, Pallas kernels, device_step(): pl.pallas_call(Kernel(n, d_model, heads, blk, hd, slots), name='decode_st...  187 us
    pallas_call x1, Pallas kernels, device_step(): pl.pallas_call(store_outputs, name='store_outputs', out_shape=tuple((jax....  4.85 us

profile of v6, /device:TPU:81, one launch (start us, length us, event | category | flops | bytes accessed | tf_op | source)
XLA Modules:
  0.0 192.2 jit_solution(12378240125822892588)
XLA Ops:
  0.6 186.7 %decode_step.1 = (bf16[1,3584]{1,0:T(2,128)(2,1)S(1)}, bf16[1,1,4096,256]{3,2,1,0:T(8,128)(2,1)S(1)}, bf16[1,1,4096,256]{3,2,1,0:T(8,128)(2,1)S(1)}, bf16[1,1,87...) custom-call(bf16[1,3584]{1,0:T(2,128)(2,1)} %hid_in.1, f32[2,128]{1,0:T(2,128)} %constant.2.clone.table_in, ...), custom_call_target="tpu_custom_call" | custom-call | tf_op jit(solution)/shard_map/decode_step/pallas_call | solution.py:555
  187.4 4.8 %store_outputs.1 = (bf16[1,3584]{1,0:T(2,128)(2,1)}, bf16[1,1,4096,256]{3,2,1,0:T(8,128)(2,1)}, bf16[1,1,4096,256]{3,2,1,0:T(8,128)(2,1)}, bf16[1,1,8704,256]{3,2,1,0:T(8,128)(2,1)}, bf16[1,1,8704,256]{3,2,1,0:T(8,128)(2,1)}) custom-call(bf16[1,3584]{1,0:T(2,128)(2,1)S(1)} %get-tuple-element.10.refs_0_, ...), custom_call_target="tpu_custom_call" | custom-call | tf_op jit(solution)/shard_map/store_outputs/pallas_call | solution.py:592

commit v7 on v6

--- a/solution.py
+++ b/solution.py
@@ -19,7 +19,7 @@
 STORE_PARTS = 2
 RELAY = 112
 HOLD = 1
-SCHEDULE = (1, 2, 3, 4, 5, 6)
+SCHEDULE = (1, 2, 3, 4, 5, 6, 7)
 NEG = -1e30
 
 
@@ -250,6 +250,11 @@
         def chip_copy(la, other, slot, i):
             return pltpu.make_async_remote_copy(src_ref=y_chip.at[la, slot], dst_ref=y_chip.at[la, slot], send_sem=ys_sem.at[la, i],
                                                 recv_sem=yr_sem.at[la, slot], device_id={"a": other * CORES + core}, device_id_type=MESH)
+
+        def pair_copy(side):
+            near = near_g if side else near_f
+            return pltpu.make_async_remote_copy(src_ref=y_chip.at[0, 2 * side], dst_ref=y_chip.at[0, 2 * side + 1], send_sem=ys_sem.at[0, side],
+                                                recv_sem=yr_sem.at[0, side], device_id={"a": near * CORES + core}, device_id_type=MESH)
 
         def half_copy(la, slot):
             return pltpu.make_async_remote_copy(src_ref=y_half.at[la, slot], dst_ref=y_half.at[la, slot], send_sem=h_sem.at[la, 0],
@@ -371,6 +376,10 @@
             y_part[la, 1] = msg[4:]
             mate_send(la).start()
             mate_send(la).wait_recv()
+            if la == 0:
+                y_chip[0, 0] = y_part[0, core] + y_mate[0]
+                pair_copy(0).start()
+                return
             y_chip[la, chip] = y_part[la, core] + y_mate[la]
             for other, i in others:
                 chip_copy(la, other, chip, i).start()
@@ -393,7 +402,7 @@
                 @pl.when(jnp.logical_or(la == 1, dst >= self.first_src))
                 def _():
                     q_send(la, dst, i).start()
-            stage(3 * la)
+            stage(4 * la)
             if la == 0:
                 for cp in w_cp[1] + kv_cp[1]:
                     cp.start()
@@ -411,7 +420,7 @@
                 for src, i in peers():
                     q_arrival(1, src).wait_recv()
                 attend_all(1, False)
-            stage(3 * la + 1)
+            stage(4 * la + 1)
             first_chip = self.first_src // CORES if la == 0 else 0
             for other, i in others:
                 @pl.when(other >= first_chip)
@@ -420,8 +429,12 @@
             out_project(la, combine(la, q, k_new, v_new, first_chip))
             if la == 0:
                 stage(2)
+                pair_copy(0).wait_recv()
+                y_chip[0, 2] = y_chip[0, 0] + y_chip[0, 1]
+                pair_copy(1).start()
+                stage(3)
             else:
-                for later in range(SCHEDULE[5], steps - HOLD):
+                for later in range(SCHEDULE[6], steps - HOLD):
                     bulk_start(later)
                 for later in range(steps - HOLD, steps):
                     bulk_start(later, slice(1, 2))
@@ -435,11 +448,15 @@
                     relay_send().wait_recv()
                     relay_forward(core, CORES - 1 - core).start()
 
-            for other, i in others:
-                chip_copy(la, other, other, i).wait_recv()
-            total = y_chip[la, 0]
-            for c in range(1, chips):
-                total = total + y_chip[la, c]
+            if la == 0:
+                pair_copy(1).wait_recv()
+                total = y_chip[0, 2] + y_chip[0, 3]
+            else:
+                for other, i in others:
+                    chip_copy(la, other, other, i).wait_recv()
+                total = y_chip[la, 0]
+                for c in range(1, chips):
+                    total = total + y_chip[la, c]
             y_half[la, core] = total
             half_copy(la, core).start()
             half_copy(la, 1 - core).wait_recv()
@@ -460,8 +477,12 @@
                 def _():
                     q_send(la, dst, i).wait_send()
             mate_send(la).wait_send()
-            for other, i in others:
-                chip_copy(la, other, chip, i).wait_send()
+            if la == 0:
+                pair_copy(0).wait_send()
+                pair_copy(1).wait_send()
+            else:
+                for other, i in others:
+                    chip_copy(la, other, chip, i).wait_send()
             half_copy(la, core).wait_send()
         p_mate_send(1).wait_send()
         for other, i in others:
@@ -523,7 +544,7 @@
             old = out[0, 0, slot:slot + 16, :].astype(jnp.float32)
             out[0, 0, slot:slot + 16, :] = jnp.where(row16 == self.seq % WINDOW - slot, new, old).astype(jnp.bfloat16)
 
-        for step in range(SCHEDULE[4], 2 * steps):
+        for step in range(SCHEDULE[5], 2 * steps):
             bulk_wait(step)
         for c in (chip, near_f, opp, near_g):
             for src_dev in ([mate] if c is chip else cores_of(c)):
@@ -581,7 +602,7 @@
                 pltpu.VMEM((2, n // CORES, 2, hd + 128), f32),
                 pltpu.VMEM((2, CORES, 4, ROW), f32),
                 pltpu.VMEM((2, 4, ROW), f32),
-                pltpu.VMEM((2, n // CORES, 4, ROW), f32),
+                pltpu.VMEM((2, 4, 4, ROW), f32),
                 pltpu.VMEM((2, CORES, 4, ROW), f32),
                 pltpu.VMEM((RELAY, hd), bf16),
                 dma((6,)), dma((16,)), dma((8,)), dma((2, 2)), dma((2, 2)), dma((2, n)), dma((2, n)), dma((2, 4)), dma((2, 2)),

time: 192 us -> 192 us (level)
  no operation moved by 1% of the time
where the time goes in v7:
time: 192 us
  Pallas kernels  191 us (99%)
    pallas_call x1, Pallas kernels, device_step(): pl.pallas_call(Kernel(n, d_model, heads, blk, hd, slots), name='decode_st...  187 us
    pallas_call x1, Pallas kernels, device_step(): pl.pallas_call(store_outputs, name='store_outputs', out_shape=tuple((jax....  4.85 us

profile of v7, /device:TPU:81, one launch (start us, length us, event | category | flops | bytes accessed | tf_op | source)
XLA Modules:
  0.0 192.0 jit_solution(12299843251716463700)
XLA Ops:
  0.6 186.5 %decode_step.1 = (bf16[1,3584]{1,0:T(2,128)(2,1)S(1)}, bf16[1,1,4096,256]{3,2,1,0:T(8,128)(2,1)S(1)}, bf16[1,1,4096,256]{3,2,1,0:T(8,128)(2,1)S(1)}, bf16[1,1,87...) custom-call(bf16[1,3584]{1,0:T(2,128)(2,1)} %hid_in.1, f32[2,128]{1,0:T(2,128)} %constant.2.clone.table_in, ...), custom_call_target="tpu_custom_call" | custom-call | tf_op jit(solution)/shard_map/decode_step/pallas_call | solution.py:576
  187.2 4.8 %store_outputs.1 = (bf16[1,3584]{1,0:T(2,128)(2,1)}, bf16[1,1,4096,256]{3,2,1,0:T(8,128)(2,1)}, bf16[1,1,4096,256]{3,2,1,0:T(8,128)(2,1)}, bf16[1,1,8704,256]{3,2,1,0:T(8,128)(2,1)}, bf16[1,1,8704,256]{3,2,1,0:T(8,128)(2,1)}) custom-call(bf16[1,3584]{1,0:T(2,128)(2,1)S(1)} %get-tuple-element.10.refs_0_, ...), custom_call_target="tpu_custom_call" | custom-call | tf_op jit(solution)/shard_map/store_outputs/pallas_call | solution.py:613

commit v8 on v6

--- a/solution.py
+++ b/solution.py
@@ -18,8 +18,7 @@
 ROW = 512
 STORE_PARTS = 2
 RELAY = 112
-HOLD = 1
-SCHEDULE = (1, 2, 3, 4, 5, 6)
+SCHEDULE = (1, 2, 3, 4, 5, 6, 7)
 NEG = -1e30
 
 
@@ -247,9 +246,10 @@
             return pltpu.make_async_remote_copy(src_ref=y_part.at[la, 1 - core], dst_ref=y_mate.at[la], send_sem=m_sem.at[la, 0],
                                                 recv_sem=m_sem.at[la, 1], device_id={"a": mate}, device_id_type=MESH)
 
-        def chip_copy(la, other, slot, i):
-            return pltpu.make_async_remote_copy(src_ref=y_chip.at[la, slot], dst_ref=y_chip.at[la, slot], send_sem=ys_sem.at[la, i],
-                                                recv_sem=yr_sem.at[la, slot], device_id={"a": other * CORES + core}, device_id_type=MESH)
+        def pair_copy(la, turn):
+            near = near_f if turn else near_g
+            return pltpu.make_async_remote_copy(src_ref=y_chip.at[la, 2 * turn], dst_ref=y_chip.at[la, 2 * turn + 1], send_sem=ys_sem.at[la, turn],
+                                                recv_sem=yr_sem.at[la, turn], device_id={"a": near * CORES + core}, device_id_type=MESH)
 
         def half_copy(la, slot):
             return pltpu.make_async_remote_copy(src_ref=y_half.at[la, slot], dst_ref=y_half.at[la, slot], send_sem=h_sem.at[la, 0],
@@ -371,9 +371,8 @@
             y_part[la, 1] = msg[4:]
             mate_send(la).start()
             mate_send(la).wait_recv()
-            y_chip[la, chip] = y_part[la, core] + y_mate[la]
-            for other, i in others:
-                chip_copy(la, other, chip, i).start()
+            y_chip[la, 0] = y_part[la, core] + y_mate[la]
+            pair_copy(la, 0).start()
 
         def stage(k):
             for step in range(SCHEDULE[k], SCHEDULE[k + 1]):
@@ -393,7 +392,7 @@
                 @pl.when(jnp.logical_or(la == 1, dst >= self.first_src))
                 def _():
                     q_send(la, dst, i).start()
-            stage(3 * la)
+            stage(4 * la)
             if la == 0:
                 for cp in w_cp[1] + kv_cp[1]:
                     cp.start()
@@ -411,7 +410,7 @@
                 for src, i in peers():
                     q_arrival(1, src).wait_recv()
                 attend_all(1, False)
-            stage(3 * la + 1)
+            stage(4 * la + 1)
             first_chip = self.first_src // CORES if la == 0 else 0
             for other, i in others:
                 @pl.when(other >= first_chip)
@@ -421,25 +420,24 @@
             if la == 0:
                 stage(2)
             else:
-                for later in range(SCHEDULE[5], steps - HOLD):
-                    bulk_start(later)
-                for later in range(steps - HOLD, steps):
-                    bulk_start(later, slice(1, 2))
+                bulk_start(steps - 1, slice(1, 2))
                 for later in range(steps, 2 * steps):
                     bulk_start(later)
-                for later in range(steps - HOLD, steps):
-                    bulk_start(later, slice(0, 1))
+            pair_copy(la, 0).wait_recv()
+            y_chip[la, 2] = y_chip[la, 0] + y_chip[la, 1]
+            pair_copy(la, 1).start()
+            if la == 0:
+                stage(3)
+            else:
+                bulk_start(steps - 1, slice(0, 1))
 
                 @pl.when(chip == relay_via)
                 def _():
                     relay_send().wait_recv()
                     relay_forward(core, CORES - 1 - core).start()
 
-            for other, i in others:
-                chip_copy(la, other, other, i).wait_recv()
-            total = y_chip[la, 0]
-            for c in range(1, chips):
-                total = total + y_chip[la, c]
+            pair_copy(la, 1).wait_recv()
+            total = y_chip[la, 2] + y_chip[la, 3]
             y_half[la, core] = total
             half_copy(la, core).start()
             half_copy(la, 1 - core).wait_recv()
@@ -460,8 +458,8 @@
                 def _():
                     q_send(la, dst, i).wait_send()
             mate_send(la).wait_send()
-            for other, i in others:
-                chip_copy(la, other, chip, i).wait_send()
+            for turn in range(2):
+                pair_copy(la, turn).wait_send()
             half_copy(la, core).wait_send()
         p_mate_send(1).wait_send()
         for other, i in others:
@@ -523,7 +521,7 @@
             old = out[0, 0, slot:slot + 16, :].astype(jnp.float32)
             out[0, 0, slot:slot + 16, :] = jnp.where(row16 == self.seq % WINDOW - slot, new, old).astype(jnp.bfloat16)
 
-        for step in range(SCHEDULE[4], 2 * steps):
+        for step in range(SCHEDULE[5], 2 * steps):
             bulk_wait(step)
         for c in (chip, near_f, opp, near_g):
             for src_dev in ([mate] if c is chip else cores_of(c)):
@@ -581,11 +579,11 @@
                 pltpu.VMEM((2, n // CORES, 2, hd + 128), f32),
                 pltpu.VMEM((2, CORES, 4, ROW), f32),
                 pltpu.VMEM((2, 4, ROW), f32),
-                pltpu.VMEM((2, n // CORES, 4, ROW), f32),
+                pltpu.VMEM((2, 4, 4, ROW), f32),
                 pltpu.VMEM((2, CORES, 4, ROW), f32),
                 pltpu.VMEM((RELAY, hd), bf16),
                 dma((6,)), dma((16,)), dma((8,)), dma((2, 2)), dma((2, 2)), dma((2, n)), dma((2, n)), dma((2, 4)), dma((2, 2)),
-                dma((2, n - 1)), dma((2, n)), dma((2, 2)), dma((2, 3)), dma((2, n // CORES)), dma((2, 2)), dma((2, 3)), dma((2, n // CORES)), dma((2, 2)), dma((4,)), pltpu.SemaphoreType.REGULAR,
+                dma((2, n - 1)), dma((2, n)), dma((2, 2)), dma((2, 3)), dma((2, n // CORES)), dma((2, 2)), dma((2, 2)), dma((2, 2)), dma((2, 2)), dma((4,)), pltpu.SemaphoreType.REGULAR,
             ],
             compiler_params=pltpu.CompilerParams(collective_id=0, has_side_effects=True, vmem_limit_bytes=48 * 2**20),
         )(hidden_in, table, loc_k, loc_v, glo_k, glo_v, loc_wq, loc_wk, loc_wv, loc_wo, loc_pre, loc_post, glo_wq, glo_wk, glo_wv, glo_wo, glo_pre, glo_post)

time: 192 us -> 192 us (level)
  no operation moved by 1% of the time
where the time goes in v8:
time: 192 us
  Pallas kernels  191 us (99%)
    pallas_call x1, Pallas kernels, device_step(): pl.pallas_call(Kernel(n, d_model, heads, blk, hd, slots), name='decode_st...  186 us
    pallas_call x1, Pallas kernels, device_step(): pl.pallas_call(store_outputs, name='store_outputs', out_shape=tuple((jax....  4.85 us

profile of v8, /device:TPU:81, one launch (start us, length us, event | category | flops | bytes accessed | tf_op | source)
XLA Modules:
  0.0 191.8 jit_solution(14031657457084764367)
XLA Ops:
  0.6 186.3 %decode_step.1 = (bf16[1,3584]{1,0:T(2,128)(2,1)S(1)}, bf16[1,1,4096,256]{3,2,1,0:T(8,128)(2,1)S(1)}, bf16[1,1,4096,256]{3,2,1,0:T(8,128)(2,1)S(1)}, bf16[1,1,87...) custom-call(bf16[1,3584]{1,0:T(2,128)(2,1)} %hid_in.1, f32[2,128]{1,0:T(2,128)} %constant.2.clone.table_in, ...), custom_call_target="tpu_custom_call" | custom-call | tf_op jit(solution)/shard_map/decode_step/pallas_call | solution.py:553
  187.0 4.8 %store_outputs.1 = (bf16[1,3584]{1,0:T(2,128)(2,1)}, bf16[1,1,4096,256]{3,2,1,0:T(8,128)(2,1)}, bf16[1,1,4096,256]{3,2,1,0:T(8,128)(2,1)}, bf16[1,1,8704,256]{3,2,1,0:T(8,128)(2,1)}, bf16[1,1,8704,256]{3,2,1,0:T(8,128)(2,1)}) custom-call(bf16[1,3584]{1,0:T(2,128)(2,1)S(1)} %get-tuple-element.10.refs_0_, ...), custom_call_target="tpu_custom_call" | custom-call | tf_op jit(solution)/shard_map/store_outputs/pallas_call | solution.py:590

commit v9 on v8

--- a/solution.py
+++ b/solution.py
@@ -17,7 +17,7 @@
 CORES = 2
 ROW = 512
 STORE_PARTS = 2
-RELAY = 112
+RELAY = 120
 SCHEDULE = (1, 2, 3, 4, 5, 6, 7)
 NEG = -1e30
 
@@ -121,7 +121,7 @@
         def loc_dst(out, src_dev, lo=0):
             if lo == 0:
                 return out.at[0, 0, pl.ds(pl.multiple_of(lax.rem(src_dev * blk, WINDOW), blk), blk)]
-            return out.at[0, 0, pl.ds(pl.multiple_of(lax.rem(src_dev * blk, WINDOW) + lo, 16), blk - lo)]
+            return out.at[0, 0, pl.ds(pl.multiple_of(lax.rem(src_dev * blk, WINDOW) + lo, 8), blk - lo)]
 
         in_cp = [pltpu.make_async_copy(hid_in, hid_b, in_sem.at[0]), pltpu.make_async_copy(table_in, table, in_sem.at[1])]
         in_cp += [pltpu.make_async_copy(g, b, in_sem.at[2 + j]) for j, (g, b) in enumerate(zip((lpre, lpost, gpre, gpost), gain_b))]

time: 192 us -> 192 us (level)
  no operation moved by 1% of the time
where the time goes in v9:
time: 192 us
  Pallas kernels  191 us (99%)
    pallas_call x1, Pallas kernels, device_step(): pl.pallas_call(Kernel(n, d_model, heads, blk, hd, slots), name='decode_st...  186 us
    pallas_call x1, Pallas kernels, device_step(): pl.pallas_call(store_outputs, name='store_outputs', out_shape=tuple((jax....  4.85 us

profile of v9, /device:TPU:81, one launch (start us, length us, event | category | flops | bytes accessed | tf_op | source)
XLA Modules:
  0.0 191.7 jit_solution(7952426200825765895)
XLA Ops:
  0.6 186.2 %decode_step.1 = (bf16[1,3584]{1,0:T(2,128)(2,1)S(1)}, bf16[1,1,4096,256]{3,2,1,0:T(8,128)(2,1)S(1)}, bf16[1,1,4096,256]{3,2,1,0:T(8,128)(2,1)S(1)}, bf16[1,1,87...) custom-call(bf16[1,3584]{1,0:T(2,128)(2,1)} %hid_in.1, f32[2,128]{1,0:T(2,128)} %constant.2.clone.table_in, ...), custom_call_target="tpu_custom_call" | custom-call | tf_op jit(solution)/shard_map/decode_step/pallas_call | solution.py:553
  186.9 4.8 %store_outputs.1 = (bf16[1,3584]{1,0:T(2,128)(2,1)}, bf16[1,1,4096,256]{3,2,1,0:T(8,128)(2,1)}, bf16[1,1,4096,256]{3,2,1,0:T(8,128)(2,1)}, bf16[1,1,8704,256]{3,2,1,0:T(8,128)(2,1)}, bf16[1,1,8704,256]{3,2,1,0:T(8,128)(2,1)}) custom-call(bf16[1,3584]{1,0:T(2,128)(2,1)S(1)} %get-tuple-element.10.refs_0_, ...), custom_call_target="tpu_custom_call" | custom-call | tf_op jit(solution)/shard_map/store_outputs/pallas_call | solution.py:590

commit v10 on v9

--- a/solution.py
+++ b/solution.py
@@ -45,7 +45,7 @@
         for p in range(STORE_PARTS):
             rows = pl.ds(p * part, part)
             copies.append(pltpu.make_async_copy(landed[j].at[0, 0, rows], outs[j].at[0, 0, rows], sem.at[j, p]))
-    for cp in copies:
+    for cp in reversed(copies):
         cp.start()
     for cp in copies:
         cp.wait()

time: 192 us -> 192 us (level)
  no operation moved by 1% of the time
where the time goes in v10:
time: 192 us
  Pallas kernels  191 us (99%)
    pallas_call x1, Pallas kernels, device_step(): pl.pallas_call(Kernel(n, d_model, heads, blk, hd, slots), name='decode_st...  186 us
    pallas_call x1, Pallas kernels, device_step(): pl.pallas_call(store_outputs, name='store_outputs', out_shape=tuple((jax....  4.82 us

profile of v10, /device:TPU:81, one launch (start us, length us, event | category | flops | bytes accessed | tf_op | source)
XLA Modules:
  0.0 191.7 jit_solution(6331739931157690661)
XLA Ops:
  0.6 186.2 %decode_step.1 = (bf16[1,3584]{1,0:T(2,128)(2,1)S(1)}, bf16[1,1,4096,256]{3,2,1,0:T(8,128)(2,1)S(1)}, bf16[1,1,4096,256]{3,2,1,0:T(8,128)(2,1)S(1)}, bf16[1,1,87...) custom-call(bf16[1,3584]{1,0:T(2,128)(2,1)} %hid_in.1, f32[2,128]{1,0:T(2,128)} %constant.2.clone.table_in, ...), custom_call_target="tpu_custom_call" | custom-call | tf_op jit(solution)/shard_map/decode_step/pallas_call | solution.py:553
  186.9 4.8 %store_outputs.1 = (bf16[1,3584]{1,0:T(2,128)(2,1)}, bf16[1,1,4096,256]{3,2,1,0:T(8,128)(2,1)}, bf16[1,1,4096,256]{3,2,1,0:T(8,128)(2,1)}, bf16[1,1,8704,256]{3,2,1,0:T(8,128)(2,1)}, bf16[1,1,8704,256]{3,2,1,0:T(8,128)(2,1)}) custom-call(bf16[1,3584]{1,0:T(2,128)(2,1)S(1)} %get-tuple-element.10.refs_0_, ...), custom_call_target="tpu_custom_call" | custom-call | tf_op jit(solution)/shard_map/store_outputs/pallas_call | solution.py:590
